TPU v7x, 32 devices: a whole 2x2x4 slice. The times are simulated.
32 devices in a mesh: dev: 32 (over z, y, x, core).
Axes of the slice: x: 2, y: 2, z: 4, core: 2. Of those that a mesh axis runs over, the one named last changes fastest.
Arguments:
- dual_blocks: bfloat16 [32, 3072, 3072], P('dev'), as said below
- rigid_modes: float32 [32, 6, 3072], P('dev'), may hold values from -5 to 5
- dual_local: float32 [32, 8, 3072], P('dev'), may hold values from -6 to 6
- coarse_rhs: float32 [32, 6, 8], P('dev'), may hold values from -4608 to 4608
- iface_sizes: int32 [32], P('dev'), may hold values from 1536 to 3072, as said below
- neighbours: int32 [32, 6], P('dev'), may hold values from -1 to 31, as said below
- shared_counts: int32 [32, 6], P('dev'), may hold values from 256 to 512, as said below
- iface_map: int32 [32, 3072], P('dev'), may hold values from -1 to 3071, as said below
- owner: int32 [32], replicated, may hold values from 0 to 31, as said below
Outputs:
- multipliers: float32 [32, 8, 3072], P('dev')
- projected_residual: float32 [32, 8, 3072], P('dev')
Inputs may be any that keep to these rules, and one draw needn't show every extreme that they name: `dual_blocks`: each block is symmetric positive definite, and so is each of its leading principal parts. Grid subdomain g is held by slot owner[g] = (g + s) mod 32 for one offset s of the draw, so the subdomains across the faces -x, +x, -y, +y, -z, +z of slot i sit in slots i - 1, i + 1, i - 4, i + 4, i - 16, i + 16, taken mod 32. `neighbours`: the subdomains form a grid of 4 x 4 x 32/16 with g = x + 4 y + 16 z. Row i lists, for the faces -x, +x, -y, +y, -z, +z of the subdomain held in slot i, the grid subdomain across that face, or -1 on the outer boundary; across a face from g the opposite face names g. `shared_counts`: equal on both sides of a shared face; some subdomain has 512 on all its faces. `iface_sizes`: the sum of the slot's shared_counts row; some subdomain has 3072. `iface_map`: for j < iface_sizes[i], entry j is f * 512 + p for the dof at position p of face f of slot i (p below that face's count), each such code once; -1 beyond. The dof at position p of a shared face pairs with the dof at position p of the opposite face of the neighbour.
All inputs are finite; a program needn't handle non-finite values.
Results may differ from a plain program's by a relative error of at most 0.025.
Values sent between devices are 32-bit elements; how exact they have to be, the bound alone decides.
No kernel may reach another device: no remote copies, remote signals or barrier semaphores. Data moves between devices by JAX's collectives and lax.ppermute only.
A program may use at most 128 MiB of HBM per device.

v0:
```python
import jax
import jax.numpy as jnp
from jax import lax
from jax.sharding import PartitionSpec as P

FACES = 6
MODES = 6
CAP = 512
NMAX = 3072
ITERS = 3


HIGHEST_PRECISION = lax.Precision.HIGHEST
OPPOSITE = (1, 0, 3, 2, 5, 4)
FACE_STEPS = (-1, 1, -4, 4, -16, 16)


def from_behind(value, axis, by):
    length = lax.axis_size(axis)
    return lax.ppermute(value, axis, [(i, (i + by) % length) for i in range(length)])


def solve_coarse(factor, vector):
    middle = lax.linalg.triangular_solve(factor, vector, left_side=True, lower=True)
    return lax.linalg.triangular_solve(factor, middle, left_side=True, lower=True, transpose_a=True)


def per_device(
    dual_blocks,
    rigid_modes,
    dual_local,
    coarse_rhs,
    iface_sizes,
    neighbours,
    shared_counts,
    iface_map,
    owner,
):
    my_slot = lax.axis_index("dev")
    devices = lax.axis_size("dev")
    loads = dual_local.shape[1]
    columns = jnp.arange(NMAX, dtype=jnp.int32)
    live_dofs = columns < iface_sizes[0]
    dof_codes = jnp.clip(jnp.where(live_dofs, iface_map[0], 0), 0, FACES * CAP - 1)
    which_face = dof_codes // CAP
    position = dof_codes % CAP
    face_row = neighbours[0]
    count_row = shared_counts[0]
    face_onehot = which_face[None, :] == jnp.arange(FACES, dtype=jnp.int32)[:, None]
    has_partner = jnp.any(face_onehot & (face_row >= 0)[:, None], axis=0)
    face_limit = jnp.sum(jnp.where(face_onehot, count_row[:, None], 0), axis=0)
    shared = live_dofs & has_partner & (position < face_limit)
    live_float = live_dofs.astype(jnp.float32)
    shared_float = shared.astype(jnp.float32)
    weights = jnp.where(shared, 0.5, live_float)
    targets = jnp.where(live_dofs, dof_codes, FACES * CAP)
    inverse = (
        jnp.full((FACES * CAP,), NMAX, jnp.int32)
        .at[targets]
        .set(columns, mode="drop")
        .reshape(FACES, CAP)
    )
    partner_slot = jnp.where(face_row >= 0, owner[jnp.clip(face_row, 0, owner.shape[0] - 1)], 0)
    face_mask = (
        (face_row >= 0)[:, None] & (jnp.arange(CAP, dtype=jnp.int32)[None, :] < count_row[:, None])
    ).astype(jnp.float32)

    def gather_faces(values):
        padded = jnp.concatenate([values, jnp.zeros((values.shape[0], 1), values.dtype)], axis=1)
        return jnp.take(padded, inverse, axis=1)

    def across_faces(face_vals, mover):
        pieces = [mover(face_vals[:, OPPOSITE[face]], -FACE_STEPS[face]) for face in range(FACES)]
        return jnp.stack(pieces, axis=1) * face_mask[None]

    def spread_back(far_faces):
        flattened = far_faces.reshape(far_faces.shape[0], FACES * CAP)
        return jnp.take(flattened, dof_codes, axis=1) * shared_float[None]

    def combine(values, far_faces):
        return live_float[None] * (values - spread_back(far_faces))

    def partial_inner(left_vec, right_vec):
        return jnp.sum(weights[None] * left_vec * right_vec, axis=1)

    modes_live = rigid_modes[0] * live_float[None]
    local_rhs = dual_local[0]
    own_modes = gather_faces(modes_live)
    own_rhs = gather_faces(local_rhs)
    setup_pieces = [
        from_behind(
            (own_modes[:, OPPOSITE[face]], own_rhs[:, OPPOSITE[face]]), "dev", -FACE_STEPS[face]
        )
        for face in range(FACES)
    ]
    far_modes = jnp.stack([piece[0] for piece in setup_pieces], axis=1) * face_mask[None]
    far_rhs = jnp.stack([piece[1] for piece in setup_pieces], axis=1) * face_mask[None]
    dual_rhs = combine(local_rhs, far_rhs)
    diagonal = lax.dot_general(
        modes_live, modes_live, (((1,), (1,)), ((), ())), precision=HIGHEST_PRECISION
    )
    coupling = -jnp.einsum("afp,bfp->afb", own_modes, far_modes, precision=HIGHEST_PRECISION)
    block_row = jnp.zeros((MODES, devices, MODES), jnp.float32).at[:, my_slot, :].set(diagonal)
    block_row = block_row.at[:, partner_slot, :].add(coupling)
    coarse_matrix, coarse_goal = (
        lax.all_gather(block_row.reshape(MODES, devices * MODES), "dev", axis=0, tiled=True),
        lax.all_gather(coarse_rhs[0], "dev", axis=0, tiled=True),
    )
    factor = jnp.linalg.cholesky(coarse_matrix)

    def modes_apply(solution):
        stacked = solution.reshape(devices, MODES, loads)
        own_part = lax.dot_general(
            stacked[my_slot], modes_live, (((0,), (0,)), ((), ())), precision=HIGHEST_PRECISION
        )
        far_part = jnp.einsum(
            "bfp,fbl->lfp", far_modes, stacked[partner_slot], precision=HIGHEST_PRECISION
        )
        return combine(own_part, far_part)

    def project(residual):
        coarse_part = lax.dot_general(
            modes_live, residual, (((1,), (1,)), ((), ())), precision=HIGHEST_PRECISION
        )
        placed = jnp.zeros((devices, MODES, loads), jnp.float32).at[my_slot].set(coarse_part)
        coarse_all = lax.psum(placed, "dev").reshape(devices * MODES, loads)
        solution = solve_coarse(factor, coarse_all)
        projected = residual - modes_apply(solution)
        norm_sq = lax.psum(partial_inner(projected, projected), "dev")
        return (projected, norm_sq)

    def dual_apply(vector):
        products = lax.dot_general(
            vector.astype(jnp.bfloat16),
            dual_blocks[0],
            (((1,), (1,)), ((), ())),
            preferred_element_type=jnp.float32,
        )
        far_part = across_faces(
            gather_faces(products), lambda piece, offset: from_behind(piece, "dev", offset)
        )
        return combine(products, far_part)

    multipliers = modes_apply(solve_coarse(factor, coarse_goal))
    residual = dual_rhs - dual_apply(multipliers)
    projected, norm_sq = project(residual)
    direction = projected
    for step_index in range(ITERS):
        applied = dual_apply(direction)
        curvature = lax.psum(partial_inner(direction, applied), "dev")
        step_size = norm_sq / curvature
        multipliers = multipliers + step_size[:, None] * direction
        residual = residual - step_size[:, None] * applied
        projected, norm_next = project(residual)
        direction = projected + (norm_next / norm_sq)[:, None] * direction
        norm_sq = norm_next
    return (multipliers[None], projected[None])


def solution(mesh):
    return jax.shard_map(
        per_device,
        mesh=mesh,
        in_specs=(
            P("dev", None, None),
            P("dev", None, None),
            P("dev", None, None),
            P("dev", None, None),
            P("dev"),
            P("dev", None),
            P("dev", None),
            P("dev", None),
            P(),
        ),
        out_specs=(P("dev", None, None), P("dev", None, None)),
        check_vma=False,
    )
```

profile of v0, /device:TPU:0, one launch (start us, length us, event | category | flops | bytes accessed | tf_op | source)
XLA Modules:
  0.0 945.3 jit_solution(9198826558787820039)
XLA Ops:
  2.1 11.8 %scatter_custom_fusion = s32[3072]{0:T(1024)S(1)} fusion(s32[3072]{0:T(1024)S(1)} %bitcast.527, s32[3072]{0:T(1024)S(1)} %iota.115, s32[]{:T(128)} %constant.261.clone.1), kind=kCustom, calls=%fused_computation.314 | custom fusion | bytes 12292 | tf_op jit(solution)/shard_map/scatter | solution.py:60
  16.0 10.9 %gather_fusion.1 = f32[3072,6]{1,0:T(8,128)} fusion(f32[6,3073]{0,1:T(8,128)S(1)} %concatenate.51, s32[3072]{0:T(1024)S(1)} %broadcast_clamp_fusion.1), kind=kCustom, calls=%fused_computation.16 | custom fusion | bytes 159744 | tf_op jit(solution)/shard_map/jit(_take)/gather | solution.py:70
  47.6 36.6 %all-gather = f32[1,192,8]{2,0,1:T(1,128)S(1)} all-gather(f32[1,6,8]{2,0,1:T(1,128)S(1)} %copy-done.67), channel_id=2, replica_groups=mesh['dev'=32] {'dev'}, dimensions={1}, use_global_device_ids=true | all-gather | bytes 6336 | tf_op jit(solution)/shard_map/all_gather | solution.py:107
  104.8 39.4 %all-gather.1 = f32[32,6,192]{2,1,0:T(8,128)S(1)} all-gather(f32[1,6,192]{2,1,0:T(8,128)S(1)} %reshape.887), channel_id=1, replica_groups=mesh['dev'=32] {'dev'}, dimensions={0}, use_global_device_ids=true | all-gather | bytes 152064 | tf_op jit(solution)/shard_map/all_gather | solution.py:106
  144.5 11.7 %cholesky.51 = f32[128,128]{1,0:T(8,128)S(1)} custom-call(f32[128,128]{1,0:T(8,128)S(1)} %cholesky.124), custom_call_target="Cholesky" | custom-call | tf_op jit(solution)/shard_map/jit(cholesky)/cholesky | solution.py:109
  175.0 19.8 %custom-call.27 = f32[2,128,128]{1,2,0:T(8,128)S(1)} custom-call(f32[2,128,128]{2,1,0:T(8,128)S(1)} %pad_maximum_fusion), custom_call_target="InvertDiagBlocksLowerTriangular" | custom-call | tf_op jit(solution)/shard_map/triangular_solve/custom-call.4 | solution.py:25
  199.3 10.9 %gather_fusion.7 = f32[3072,8]{1,0:T(8,128)} fusion(f32[8,3072]{0,1:T(8,128)S(1)} %copy.143, s32[3072]{0:T(1024)S(1)} %get-tuple-element.216), kind=kCustom, calls=%fused_computation.clone | custom fusion | bytes 208896 | tf_op jit(solution)/shard_map/jit(_take)/gather | solution.py:78
  212.9 12.0 %fusion.6 = f32[8,3072]{1,0:T(8,128)} fusion(bf16[1,3072,3072]{2,1,0:T(8,128)(2,1)} %param.27, f32[8,3072]{1,0:T(8,128)S(1)} %fusion.17), kind=kOutput, calls=%fused_computation.30 | convolution fusion | flops 151019520 | bytes 19070976 | tf_op jit(solution)/shard_map/dot_general | solution.py:133
  277.0 12.6 %gather_fusion.11 = f32[3072,8]{1,0:T(8,128)} fusion(f32[8,3072]{0,1:T(8,128)} %get-tuple-element.205, s32[3072]{0:T(1024)S(1)} %get-tuple-element.216), kind=kCustom, calls=%fused_computation.3.clone | custom fusion | bytes 208896 | tf_op jit(solution)/shard_map/jit(_take)/gather | solution.py:78
  292.1 10.9 %gather_fusion.9 = f32[3072,8]{1,0:T(8,128)} fusion(f32[8,3072]{0,1:T(8,128)S(1)} %copy-done.2, s32[3072]{0:T(1024)S(1)} %get-tuple-element.216), kind=kCustom, calls=%fused_computation.2.clone | custom fusion | bytes 208896 | tf_op jit(solution)/shard_map/jit(_take)/gather | solution.py:78
  309.1 37.8 %psum.70 = f32[192,8]{0,1:T(8,128)S(1)} all-reduce(f32[192,8]{0,1:T(8,128)S(1)} %reshape.519), channel_id=1, replica_groups=mesh['dev'=32] {'dev'}, use_global_device_ids=true, to_apply=%region_10.15 | all-reduce | flops 1536 | bytes 12288 | tf_op jit(solution)/shard_map/psum | solution.py:126
  353.6 10.9 %gather_fusion.12 = f32[3072,8]{1,0:T(8,128)} fusion(f32[8,3072]{0,1:T(8,128)S(1)} %copy.157, s32[3072]{0:T(1024)S(1)} %get-tuple-element.216), kind=kCustom, calls=%fused_computation.4.clone | custom fusion | bytes 208896 | tf_op jit(solution)/shard_map/jit(_take)/gather | solution.py:78
  366.6 12.0 %fusion.4 = f32[8,3072]{1,0:T(8,128)} fusion(bf16[1,3072,3072]{2,1,0:T(8,128)(2,1)} %param.27, f32[8,3072]{1,0:T(8,128)S(1)} %fusion.16), kind=kOutput, calls=%fused_computation.28 | convolution fusion | flops 151019520 | bytes 19070976 | tf_op jit(solution)/shard_map/dot_general | solution.py:133
  381.3 11.0 %gather_fusion.13 = f32[3072,8]{1,0:T(8,128)S(1)} fusion(f32[8,3073]{0,1:T(8,128)} %concatenate.55.clone, s32[3072]{0:T(1024)} %copy-done.45), kind=kCustom, calls=%fused_computation.12.clone | custom fusion | bytes 208896 | tf_op jit(solution)/shard_map/jit(_take)/gather | solution.py:70
  414.7 13.8 %gather_fusion.14 = f32[3072,8]{1,0:T(8,128)} fusion(f32[8,3072]{0,1:T(8,128)} %bitcast_multiply_fusion.2, s32[3072]{0:T(1024)} %copy-done.34), kind=kCustom, calls=%fused_computation.5.clone | custom fusion | bytes 208896 | tf_op jit(solution)/shard_map/jit(_take)/gather | solution.py:78
  430.6 38.5 %all-reduce.11 = (f32[8]{0:T(128)S(1)}, f32[8]{0:T(128)S(1)}) all-reduce(f32[8]{0:T(128)S(1)} %get-tuple-element.155, f32[8]{0:T(128)S(1)} %get-tuple-element.154), channel_id=1, replica_groups=mesh['dev'=32] {'dev'}, use_global_device_ids=true, to_apply=%region_12.17 | all-reduce | flops 16 | bytes 128 | tf_op jit(solution)/shard_map/psum | solution.py:129
  473.3 39.3 %psum.73 = f32[192,8]{0,1:T(8,128)S(1)} all-reduce(f32[192,8]{0,1:T(8,128)S(1)} %reshape.523), channel_id=1, replica_groups=mesh['dev'=32] {'dev'}, use_global_device_ids=true, to_apply=%region_15.20 | all-reduce | flops 1536 | bytes 12288 | tf_op jit(solution)/shard_map/psum | solution.py:126
  518.6 10.9 %gather_fusion.15 = f32[3072,8]{1,0:T(8,128)} fusion(f32[8,3072]{0,1:T(8,128)S(1)} %copy.167, s32[3072]{0:T(1024)S(1)} %copy-done.35), kind=kCustom, calls=%fused_computation.6.clone | custom fusion | bytes 208896 | tf_op jit(solution)/shard_map/jit(_take)/gather | solution.py:78
  531.8 40.7 %psum.74 = f32[8]{0:T(128)S(1)} all-reduce(f32[8]{0:T(128)S(1)} %get-tuple-element.210), channel_id=1, replica_groups=mesh['dev'=32] {'dev'}, use_global_device_ids=true, to_apply=%region_17.22 | all-reduce | flops 8 | bytes 64 | tf_op jit(solution)/shard_map/psum | solution.py:129
  573.2 12.0 %fusion.2 = f32[8,3072]{1,0:T(8,128)} fusion(bf16[1,3072,3072]{2,1,0:T(8,128)(2,1)} %param.27, f32[8,3072]{1,0:T(8,128)S(1)} %multiply_add_fusion.1), kind=kOutput, calls=%fused_computation.26 | convolution fusion | flops 151019520 | bytes 19070976 | tf_op jit(solution)/shard_map/dot_general | solution.py:133
  587.9 11.0 %gather_fusion.16 = f32[3072,8]{1,0:T(8,128)S(1)} fusion(f32[8,3073]{0,1:T(8,128)} %concatenate.56.clone, s32[3072]{0:T(1024)} %copy-done.45), kind=kCustom, calls=%fused_computation.13.clone | custom fusion | bytes 208896 | tf_op jit(solution)/shard_map/jit(_take)/gather | solution.py:70
  621.4 13.4 %gather_fusion.17 = f32[3072,8]{1,0:T(8,128)} fusion(f32[8,3072]{0,1:T(8,128)} %bitcast_multiply_fusion.1, s32[3072]{0:T(1024)} %copy-done.34), kind=kCustom, calls=%fused_computation.7.clone | custom fusion | bytes 208896 | tf_op jit(solution)/shard_map/jit(_take)/gather | solution.py:78
  636.9 38.5 %psum.75 = f32[8]{0:T(128)S(1)} all-reduce(f32[8]{0:T(128)S(1)} %multiply_reduce_fusion.1), channel_id=1, replica_groups=mesh['dev'=32] {'dev'}, use_global_device_ids=true, to_apply=%region_19.24 | all-reduce | flops 8 | bytes 64 | tf_op jit(solution)/shard_map/psum | solution.py:150
  679.7 39.3 %psum.76 = f32[192,8]{0,1:T(8,128)S(1)} all-reduce(f32[192,8]{0,1:T(8,128)S(1)} %reshape.527), channel_id=1, replica_groups=mesh['dev'=32] {'dev'}, use_global_device_ids=true, to_apply=%region_20.25 | all-reduce | flops 1536 | bytes 12288 | tf_op jit(solution)/shard_map/psum | solution.py:126
  725.5 11.9 %gather_fusion.18 = f32[3072,8]{1,0:T(8,128)} fusion(f32[8,3072]{0,1:T(8,128)S(1)} %copy.177, s32[3072]{0:T(1024)} %copy-done.34), kind=kCustom, calls=%fused_computation.8.clone | custom fusion | bytes 208896 | tf_op jit(solution)/shard_map/jit(_take)/gather | solution.py:78
  739.8 40.8 %psum.77 = f32[8]{0:T(128)S(1)} all-reduce(f32[8]{0:T(128)S(1)} %get-tuple-element.212), channel_id=1, replica_groups=mesh['dev'=32] {'dev'}, use_global_device_ids=true, to_apply=%region_22.27 | all-reduce | flops 8 | bytes 64 | tf_op jit(solution)/shard_map/psum | solution.py:129
  781.1 12.0 %fusion = f32[8,3072]{1,0:T(8,128)} fusion(bf16[1,3072,3072]{2,1,0:T(8,128)(2,1)} %param.27, f32[8,3072]{1,0:T(8,128)S(1)} %get-tuple-element.213, f32[8,3072]{1,0:T(8,128)S(1)} %multiply_add_fusion.1, f32[8]{0:T(128)S(1)} %div.44), kind=kOutput, calls=%fused_computation.24 | convolution fusion | flops 151068672 | bytes 19169312 | tf_op jit(solution)/shard_map/dot_general | solution.py:133
  795.8 11.0 %gather_fusion.19 = f32[3072,8]{1,0:T(8,128)S(1)} fusion(f32[8,3073]{0,1:T(8,128)} %concatenate.57.clone, s32[3072]{0:T(1024)} %copy-done.45), kind=kCustom, calls=%fused_computation.14.clone | custom fusion | bytes 208896 | tf_op jit(solution)/shard_map/jit(_take)/gather | solution.py:70
  829.2 13.5 %gather_fusion.20 = f32[3072,8]{1,0:T(8,128)} fusion(f32[8,3072]{0,1:T(8,128)} %bitcast_multiply_fusion, s32[3072]{0:T(1024)} %copy-done.34), kind=kCustom, calls=%fused_computation.9.clone | custom fusion | bytes 208896 | tf_op jit(solution)/shard_map/jit(_take)/gather | solution.py:78
  844.8 38.5 %psum.78 = f32[8]{0:T(128)S(1)} all-reduce(f32[8]{0:T(128)S(1)} %get-tuple-element.158), channel_id=1, replica_groups=mesh['dev'=32] {'dev'}, use_global_device_ids=true, to_apply=%region_24.29 | all-reduce | flops 8 | bytes 64 | tf_op jit(solution)/shard_map/psum | solution.py:150
  887.7 39.3 %psum.79 = f32[192,8]{0,1:T(8,128)S(1)} all-reduce(f32[192,8]{0,1:T(8,128)S(1)} %reshape.531), channel_id=1, replica_groups=mesh['dev'=32] {'dev'}, use_global_device_ids=true, to_apply=%region_25.30 | all-reduce | flops 1536 | bytes 12288 | tf_op jit(solution)/shard_map/psum | solution.py:126
  931.5 10.9 %gather_fusion.21 = f32[3072,8]{1,0:T(8,128)} fusion(f32[8,3072]{0,1:T(8,128)S(1)} %copy.187, s32[3072]{0:T(1024)S(1)} %copy-done.36), kind=kCustom, calls=%fused_computation.10.clone | custom fusion | bytes 208896 | tf_op jit(solution)/shard_map/jit(_take)/gather | solution.py:78
  (487 shorter events, 257.4 us)
Async XLA Ops:
  29.5 67.2 %collective-permute-start = (f32[6,512]{1,0:T(8,128)}, f32[6,512]{1,0:T(8,128)}, u32[]{:S(2)}, u32[]{:S(2)}) collective-permute-start(f32[6,512]{1,0:T(8,128)} %get-tuple-element.199), channel_id=1, source_target_pairs={{0,1},{1,2},{2,3},{3,4},{4,5},{5,6},{6,7},{7,8},{8,9},{9,10},{10,1... | collective-permute-start | bytes 36872 | tf_op jit(solution)/shard_map/ppermute | solution.py:20
  30.0 67.4 %collective-permute-start.1 = (f32[6,512]{1,0:T(8,128)}, f32[6,512]{1,0:T(8,128)}, u32[]{:S(2)}, u32[]{:S(2)}) collective-permute-start(f32[6,512]{1,0:T(8,128)} %get-tuple-element.198), channel_id=1, source_target_pairs={{0,31},{1,0},{2,1},{3,2},{4,3},{5,4},{6,5},{7,6},{8,7},{9,8},{10,9... | collective-permute-start | bytes 36872 | tf_op jit(solution)/shard_map/ppermute | solution.py:20
  36.0 62.2 %collective-permute-start.2 = (f32[6,512]{1,0:T(8,128)}, f32[6,512]{1,0:T(8,128)}, u32[]{:S(2)}, u32[]{:S(2)}) collective-permute-start(f32[6,512]{1,0:T(8,128)} %get-tuple-element.197), channel_id=1, source_target_pairs={{0,4},{1,5},{2,6},{3,7},{4,8},{5,9},{6,10},{7,11},{8,12},{9,13},{1... | collective-permute-start | bytes 36872 | tf_op jit(solution)/shard_map/ppermute | solution.py:20
  36.0 62.9 %collective-permute-start.3 = (f32[6,512]{1,0:T(8,128)}, f32[6,512]{1,0:T(8,128)}, u32[]{:S(2)}, u32[]{:S(2)}) collective-permute-start(f32[6,512]{1,0:T(8,128)} %get-tuple-element.196), channel_id=1, source_target_pairs={{0,28},{1,29},{2,30},{3,31},{4,0},{5,1},{6,2},{7,3},{8,4},{9,5},{1... | collective-permute-start | bytes 36872 | tf_op jit(solution)/shard_map/ppermute | solution.py:20
  40.7 58.9 %collective-permute-start.4 = (f32[6,512]{1,0:T(8,128)}, f32[6,512]{1,0:T(8,128)}, u32[]{:S(2)}, u32[]{:S(2)}) collective-permute-start(f32[6,512]{1,0:T(8,128)} %get-tuple-element.195), channel_id=1, source_target_pairs={{0,16},{1,17},{2,18},{3,19},{4,20},{5,21},{6,22},{7,23},{8,24},{9,... | collective-permute-start | bytes 36872 | tf_op jit(solution)/shard_map/ppermute | solution.py:20
  239.2 10.1 %collective-permute-start.6 = (f32[8,512]{1,0:T(8,128)S(1)}, f32[8,512]{1,0:T(8,128)S(1)}, u32[]{:S(2)}, u32[]{:S(2)}) collective-permute-start(f32[8,512]{1,0:T(8,128)S(1)} %get-tuple-element.187), channel_id=1, source_target_pairs={{0,1},{1,2},{2,3},{3,4},{4,5},{5,6},{6,7},{7,8},{8,9},{9,10},{10,1... | collective-permute-start | bytes 49160 | tf_op jit(solution)/shard_map/ppermute | solution.py:20
  239.6 18.3 %collective-permute-start.7 = (f32[8,512]{1,0:T(8,128)S(1)}, f32[8,512]{1,0:T(8,128)S(1)}, u32[]{:S(2)}, u32[]{:S(2)}) collective-permute-start(f32[8,512]{1,0:T(8,128)S(1)} %get-tuple-element.186), channel_id=1, source_target_pairs={{0,31},{1,0},{2,1},{3,2},{4,3},{5,4},{6,5},{7,6},{8,7},{9,8},{10,9... | collective-permute-start | bytes 49160 | tf_op jit(solution)/shard_map/ppermute | solution.py:20
  244.6 13.4 %collective-permute-start.8 = (f32[8,512]{1,0:T(8,128)S(1)}, f32[8,512]{1,0:T(8,128)S(1)}, u32[]{:S(2)}, u32[]{:S(2)}) collective-permute-start(f32[8,512]{1,0:T(8,128)S(1)} %get-tuple-element.185), channel_id=1, source_target_pairs={{0,4},{1,5},{2,6},{3,7},{4,8},{5,9},{6,10},{7,11},{8,12},{9,13},{1... | collective-permute-start | bytes 49160 | tf_op jit(solution)/shard_map/ppermute | solution.py:20
  244.6 13.4 %collective-permute-start.9 = (f32[8,512]{1,0:T(8,128)S(1)}, f32[8,512]{1,0:T(8,128)S(1)}, u32[]{:S(2)}, u32[]{:S(2)}) collective-permute-start(f32[8,512]{1,0:T(8,128)S(1)} %get-tuple-element.184), channel_id=1, source_target_pairs={{0,28},{1,29},{2,30},{3,31},{4,0},{5,1},{6,2},{7,3},{8,4},{9,5},{1... | collective-permute-start | bytes 49160 | tf_op jit(solution)/shard_map/ppermute | solution.py:20
  249.3 13.4 %collective-permute-start.10 = (f32[8,512]{1,0:T(8,128)S(1)}, f32[8,512]{1,0:T(8,128)S(1)}, u32[]{:S(2)}, u32[]{:S(2)}) collective-permute-start(f32[8,512]{1,0:T(8,128)S(1)} %get-tuple-element.183), channel_id=1, source_target_pairs={{0,16},{1,17},{2,18},{3,19},{4,20},{5,21},{6,22},{7,23},{8,24},{9,... | collective-permute-start | bytes 49160 | tf_op jit(solution)/shard_map/ppermute | solution.py:20
  249.3 6.8 collective-permute-start.12
  256.1 6.6 collective-permute-start.11
  257.9 7.8 collective-permute-start.13
  257.9 8.3 collective-permute-start.14
  258.0 8.9 collective-permute-start.15
  262.7 6.7 collective-permute-start.17
  394.3 10.1 %collective-permute-start.18 = (f32[8,512]{1,0:T(8,128)S(1)}, f32[8,512]{1,0:T(8,128)S(1)}, u32[]{:S(2)}, u32[]{:S(2)}) collective-permute-start(f32[8,512]{1,0:T(8,128)S(1)} %get-tuple-element.181), channel_id=1, source_target_pairs={{0,1},{1,2},{2,3},{3,4},{4,5},{5,6},{6,7},{7,8},{8,9},{9,10},{10,1... | collective-permute-start | bytes 49160 | tf_op jit(solution)/shard_map/ppermute | solution.py:20
  394.4 13.6 %collective-permute-start.19 = (f32[8,512]{1,0:T(8,128)S(1)}, f32[8,512]{1,0:T(8,128)S(1)}, u32[]{:S(2)}, u32[]{:S(2)}) collective-permute-start(f32[8,512]{1,0:T(8,128)S(1)} %get-tuple-element.180), channel_id=1, source_target_pairs={{0,31},{1,0},{2,1},{3,2},{4,3},{5,4},{6,5},{7,6},{8,7},{9,8},{10,9... | collective-permute-start | bytes 49160 | tf_op jit(solution)/shard_map/ppermute | solution.py:20
  399.7 8.9 collective-permute-start.20
  399.7 9.5 %collective-permute-start.21 = (f32[8,512]{1,0:T(8,128)S(1)}, f32[8,512]{1,0:T(8,128)S(1)}, u32[]{:S(2)}, u32[]{:S(2)}) collective-permute-start(f32[8,512]{1,0:T(8,128)S(1)} %get-tuple-element.178), channel_id=1, source_target_pairs={{0,28},{1,29},{2,30},{3,31},{4,0},{5,1},{6,2},{7,3},{8,4},{9,5},{1... | collective-permute-start | bytes 49160 | tf_op jit(solution)/shard_map/ppermute | solution.py:20
  404.4 5.9 collective-permute-start.23
  600.8 10.3 %collective-permute-start.24 = (f32[8,512]{1,0:T(8,128)S(1)}, f32[8,512]{1,0:T(8,128)S(1)}, u32[]{:S(2)}, u32[]{:S(2)}) collective-permute-start(f32[8,512]{1,0:T(8,128)S(1)} %get-tuple-element.175), channel_id=1, source_target_pairs={{0,1},{1,2},{2,3},{3,4},{4,5},{5,6},{6,7},{7,8},{8,9},{9,10},{10,1... | collective-permute-start | bytes 49160 | tf_op jit(solution)/shard_map/ppermute | solution.py:20
  600.9 13.7 %collective-permute-start.25 = (f32[8,512]{1,0:T(8,128)S(1)}, f32[8,512]{1,0:T(8,128)S(1)}, u32[]{:S(2)}, u32[]{:S(2)}) collective-permute-start(f32[8,512]{1,0:T(8,128)S(1)} %get-tuple-element.174), channel_id=1, source_target_pairs={{0,31},{1,0},{2,1},{3,2},{4,3},{5,4},{6,5},{7,6},{8,7},{9,8},{10,9... | collective-permute-start | bytes 49160 | tf_op jit(solution)/shard_map/ppermute | solution.py:20
  606.2 9.0 collective-permute-start.26
  606.2 9.6 %collective-permute-start.27 = (f32[8,512]{1,0:T(8,128)S(1)}, f32[8,512]{1,0:T(8,128)S(1)}, u32[]{:S(2)}, u32[]{:S(2)}) collective-permute-start(f32[8,512]{1,0:T(8,128)S(1)} %get-tuple-element.172), channel_id=1, source_target_pairs={{0,28},{1,29},{2,30},{3,31},{4,0},{5,1},{6,2},{7,3},{8,4},{9,5},{1... | collective-permute-start | bytes 49160 | tf_op jit(solution)/shard_map/ppermute | solution.py:20
  611.1 5.9 collective-permute-start.29
  808.8 10.1 %collective-permute-start.30 = (f32[8,512]{1,0:T(8,128)S(1)}, f32[8,512]{1,0:T(8,128)S(1)}, u32[]{:S(2)}, u32[]{:S(2)}) collective-permute-start(f32[8,512]{1,0:T(8,128)S(1)} %get-tuple-element.169), channel_id=1, source_target_pairs={{0,1},{1,2},{2,3},{3,4},{4,5},{5,6},{6,7},{7,8},{8,9},{9,10},{10,1... | collective-permute-start | bytes 49160 | tf_op jit(solution)/shard_map/ppermute | solution.py:20
  808.8 13.6 %collective-permute-start.31 = (f32[8,512]{1,0:T(8,128)S(1)}, f32[8,512]{1,0:T(8,128)S(1)}, u32[]{:S(2)}, u32[]{:S(2)}) collective-permute-start(f32[8,512]{1,0:T(8,128)S(1)} %get-tuple-element.168), channel_id=1, source_target_pairs={{0,31},{1,0},{2,1},{3,2},{4,3},{5,4},{6,5},{7,6},{8,7},{9,8},{10,9... | collective-permute-start | bytes 49160 | tf_op jit(solution)/shard_map/ppermute | solution.py:20
  814.2 8.9 collective-permute-start.32
  814.2 9.5 %collective-permute-start.33 = (f32[8,512]{1,0:T(8,128)S(1)}, f32[8,512]{1,0:T(8,128)S(1)}, u32[]{:S(2)}, u32[]{:S(2)}) collective-permute-start(f32[8,512]{1,0:T(8,128)S(1)} %get-tuple-element.166), channel_id=1, source_target_pairs={{0,28},{1,29},{2,30},{3,31},{4,0},{5,1},{6,2},{7,3},{8,4},{9,5},{1... | collective-permute-start | bytes 49160 | tf_op jit(solution)/shard_map/ppermute | solution.py:20
  818.9 5.3 collective-permute-start.34
  818.9 5.9 collective-permute-start.35
  (86 other events, 3273.6 us)
where the time goes:
time: 954 us; the launch traced here: 945 us
  blocking collectives  429 us (45%)
  local copies, waits for them, and re-layouts  283 us (30%)
  matrix products  80.1 us (8%)
  other arithmetic  72 us (8%)
  starting transfers between devices  69.4 us (7%)
    psum x4, blocking collectives, project(): coarse_all = lax.psum(placed, 'dev').reshape(devices * MODES, loads)  156 us
    gather x20, local copies, waits for them, and re-layouts, spread_back(): return jnp.take(flattened, dof_codes, axis=1) * shared_float[None]  139 us
    psum x3, blocking collectives, project(): norm_sq = lax.psum(partial_inner(projected, projected), 'dev')  120 us
    psum x2, blocking collectives, per_device(): curvature = lax.psum(partial_inner(direction, applied), 'dev')  77 us
    gather x12, local copies, waits for them, and re-layouts, gather_faces(): return jnp.take(padded, inverse, axis=1)  70.2 us
    ppermute x36, starting transfers between devices, from_behind(): lax.ppermute(value, axis, [(i, (i + by) % length) for i in range(length)])  69.4 us
    dot_general x4, matrix products, dual_apply(): lax.dot_general(vector.astype(jnp.bfloat16), dual_blocks[0], (((1,), (1,)...  47.9 us
    all_gather x1, blocking collectives, per_device(): lax.all_gather(block_row.reshape(MODES, devices * MODES), 'dev', axis=0,...  39.4 us
  transfers between devices with their start and end apart: 36, of which 2 were waited for; matrix products, arithmetic and copies ran while one was open for 4% of the time, Pallas kernels for 0%

commit v1 on v0

v1 whole, which is shorter than its diff:
```python
import functools

import jax
import jax.numpy as jnp
from jax import lax
from jax.experimental import pallas as pl
from jax.experimental.pallas import tpu as pltpu
from jax.sharding import PartitionSpec as P

HI = lax.Precision.HIGHEST
F32 = jnp.float32
STEPS = (-1, 1, -4, 4, -16, 16)
LANES = 128
PAD = 8
EXTRA = 64
SLOT, SHIFT, SIZE, COUNT, LINK = 0, 1, 2, 3, 9


def pairings(n):
    out = []
    for axis, dist in enumerate((1, 4, 16)):
        seen = []
        for phase in (0, 1):
            pairs = sorted({tuple(sorted((i, (i + dist) % n))) for i in range(n) if (i // dist) % 2 == phase})
            if pairs in seen:
                continue
            seen.append(pairs)
            out.append((axis, phase, pairs + [(j, i) for i, j in pairs]))
    merged = [sum(1 for a, _, _ in out if a == axis) == 1 for axis in range(3)]
    return out, merged


def dot(a, b, dims=((1,), (0,)), precision=HI):
    return lax.dot_general(a, b, (dims, ((), ())), precision=precision, preferred_element_type=F32)


def iota(shape, dim):
    return lax.broadcasted_iota(jnp.int32, shape, dim)


def take(x, idx):
    return jnp.take_along_axis(x, idx, axis=1, mode="promise_in_bounds")


def permute(load, table, blocks):
    tiles = [load(b) for b in range(blocks)]
    out = []
    for b in range(blocks):
        row = jnp.broadcast_to(table[b : b + 1, :], (8, LANES))
        high, low = row >> 7, row & 127
        acc = jnp.zeros((8, LANES), F32)
        for s in range(blocks):
            acc = jnp.where(high == s, take(tiles[s], low), acc)
        out.append(acc)
    return out


def tile_of(ref):
    return lambda b: ref[:, b * LANES : (b + 1) * LANES]


class Faces:
    def __init__(self, sc, n, cap):
        self.sc, self.n, self.cap = sc, n, cap
        self.per = cap // LANES
        self.list, self.merged = pairings(n)

    def bit(self, axis):
        return (self.sc[SLOT] >> (0, 2, 4)[axis]) & 1

    def live(self, f, t):
        return iota((8, LANES), 1) + t * LANES < self.sc[COUNT + f]

    def shared(self, f, t):
        return self.live(f, t) & (self.sc[LINK + f] > 0)

    def send(self, tiles, outs):
        for ref, (axis, phase, _) in zip(outs, self.list):
            up = self.sc[LINK + 2 * axis + 1] > 0 if self.merged[axis] else self.bit(axis) == phase
            for t in range(self.per):
                low, high = tiles[2 * axis * self.per + t], tiles[(2 * axis + 1) * self.per + t]
                ref[:, t * LANES : (t + 1) * LANES] = jnp.where(up, high, low)

    def far(self, ins, f, t):
        axis = f // 2
        mine = [ref for ref, (a, _, _) in zip(ins, self.list) if a == axis]
        vals = [ref[:, t * LANES : (t + 1) * LANES] for ref in mine]
        if len(vals) == 1:
            v = vals[0]
        else:
            zero = self.bit(axis) == 0
            v = jnp.where(zero, vals[0], vals[1]) if f % 2 else jnp.where(zero, vals[1], vals[0])
        return jnp.where(self.shared(f, t), v, 0.0)


def spread(n, width):
    row, col = iota((LANES, width), 0), iota((LANES, width), 1)
    hit = jnp.zeros((LANES, width), jnp.bool_)
    for b, step in enumerate((0,) + STEPS):
        hit = hit | ((row >> 3 == b) & (col == (step % n) * PAD + (row & 7)))
    return jnp.where(hit, 1.0, 0.0).astype(F32)


def prepare_kernel(n, cap, faces, sc, map_row, map_tile, modes, rhs, *refs):
    nm = len(pairings(n)[0])
    modes_out, rhs_out, code_out, inv_out = refs[:4]
    sends, scratch = refs[4 : 4 + nm], refs[4 + nm]
    nmax = cap * faces
    blocks = nmax // LANES
    size = sc[SIZE]
    j = iota((1, nmax), 1)
    code = jnp.where(j < size, map_row[...], -1)
    place = j + 1
    high, low = code >> 7, code & 127
    rows = -(-blocks // 8) * 8
    group = iota((rows, nmax), 0)
    hit = jnp.broadcast_to(high, (rows, nmax)) == group
    left = jnp.concatenate(
        [
            jnp.where(hit, jnp.broadcast_to(place >> 6, (rows, nmax)), 0).astype(F32),
            jnp.where(hit, jnp.broadcast_to(place & 63, (rows, nmax)), 0).astype(F32),
        ],
        axis=0,
    ).astype(jnp.bfloat16)
    right = jnp.where(jnp.broadcast_to(low, (LANES, nmax)) == iota((LANES, nmax), 0), 1.0, 0.0).astype(jnp.bfloat16)
    both = dot(left, right, ((1,), (1,)), None)
    inv = (both[:rows] * 64.0 + both[rows:]).astype(jnp.int32) - 1
    inv_out[...] = inv[:blocks]
    tile_j = iota((blocks, LANES), 0) * LANES + iota((blocks, LANES), 1)
    code_out[...] = jnp.where(tile_j < size, map_tile[...], -1)
    scratch[...] = jnp.zeros_like(scratch)
    scratch[: modes.shape[1], :] = modes[0]
    moved = permute(tile_of(scratch), inv_out, blocks)
    for b, v in enumerate(moved):
        modes_out[:, b * LANES : (b + 1) * LANES] = v
    Faces(sc, n, cap).send(moved, sends)
    for b, v in enumerate(permute(lambda b: rhs[0, :, b * LANES : (b + 1) * LANES], inv_out, blocks)):
        rhs_out[:, b * LANES : (b + 1) * LANES] = v


def row_kernel(n, cap, faces, sc, modes, goal, *refs):
    nm = len(pairings(n)[0])
    ins, (c_out, tile_out) = refs[:nm], refs[nm:]
    fc = Faces(sc, n, cap)
    c_out[...] = jnp.zeros_like(c_out)
    c_out[0:PAD, :] = modes[...]
    for f in range(faces):
        for t in range(fc.per):
            at = f * cap + t * LANES
            c_out[PAD * (1 + f) : PAD * (2 + f), at : at + LANES] = -fc.far(ins, f, t)
    row = dot(modes[...], c_out[...], ((1,), (1,)))
    tile = jnp.concatenate([row, jnp.zeros((8, LANES - EXTRA), F32)], axis=1) + goal[...]
    for i in range(n):
        tile_out[i] = tile


def sweep(ref, side):
    cols = side // LANES
    reals = 6

    def step(b, carry):
        at = pl.multiple_of(b * PAD, PAD)
        column = pl.multiple_of((at // LANES) * LANES, LANES)
        lane0 = at - column
        sub, lane = iota((8, LANES), 0), iota((8, LANES), 1)
        rows = [ref[pl.ds(at, PAD), j * LANES : (j + 1) * LANES] for j in range(cols)]
        pivot = ref[pl.ds(at, PAD), pl.ds(column, LANES)]
        g = [take(pivot, jnp.full((8, LANES), 0, jnp.int32) + (lane0 + c)) for c in range(reals)]
        for k in range(reals):
            top = [jnp.broadcast_to(g[c][k : k + 1, :], (8, LANES)) for c in range(reals)]
            inv = 1.0 / top[k]
            mine = sub == k
            new = []
            for c in range(reals):
                if c == k:
                    new.append(jnp.where(mine, inv, -g[k] * inv))
                else:
                    scaled = top[c] * inv
                    new.append(jnp.where(mine, scaled, g[c] - g[k] * scaled))
            g = new
        w = []
        for j in range(cols):
            acc = jnp.zeros((8, LANES), F32)
            for c in range(reals):
                acc = acc + g[c] * jnp.broadcast_to(rows[j][c : c + 1, :], (8, LANES))
            here = (lane + j * LANES >= at) & (lane + j * LANES < at + reals)
            minus = acc
            for c in range(reals):
                minus = jnp.where(lane + j * LANES == at + c, -g[c], minus)
            w.append((minus, here))
        wb = [[jnp.broadcast_to(w[j][0][c : c + 1, :], (8, LANES)) for c in range(reals)] for j in range(cols)]
        for i in range(side // PAD):
            r = slice(i * PAD, (i + 1) * PAD)
            src = ref[r, pl.ds(column, LANES)]
            splat = [take(src, jnp.full((8, LANES), 0, jnp.int32) + (lane0 + c)) for c in range(reals)]
            for j in range(cols):
                x = jnp.where(w[j][1], 0.0, ref[r, j * LANES : (j + 1) * LANES])
                for c in range(reals):
                    x = x - splat[c] * wb[j][c]
                ref[r, j * LANES : (j + 1) * LANES] = x
        for j in range(cols):
            ref[pl.ds(at, PAD), j * LANES : (j + 1) * LANES] = jnp.where(sub < reals, w[j][0], rows[j])
        return carry

    lax.fori_loop(0, side // PAD, step, 0)


def place(tile, src, dst, width=PAD):
    moved = tile if src == dst else pltpu.roll(tile, (dst - src) % LANES, 1)
    lane = iota((8, LANES), 1)
    return jnp.where((lane >= dst) & (lane < dst + width), moved, 0.0)


def invert(n, sc, recv, dred, qrb, sbb):
    half = n // 2
    side = half * PAD
    cols = side // LANES
    shift = sc[SHIFT]
    layers = n // 16
    qrb[...] = jnp.zeros_like(qrb)
    sbb[...] = jnp.zeros_like(sbb)
    dred[...] = jnp.zeros_like(dred)
    for g in range(n):
        x, y, z = g % 4, g // 4 % 4, g // 16
        k = g // 2
        tile = recv[lax.rem(g + shift, n)]
        at = k * PAD
        own = slice((at // LANES) * LANES, (at // LANES + 1) * LANES)
        diag = place(tile, 0, at % LANES)
        if (x + y + z) % 2 == 0:
            dred[:, own] += diag
            there = (x > 0, x < 3, y > 0, y < 3, z > 0, z < layers - 1)
            parts = {}
            for f, step in enumerate(STEPS):
                if there[f]:
                    to = (g + step) // 2 * PAD
                    piece = place(tile, PAD * (1 + f), to % LANES)
                    parts[to // LANES] = parts[to // LANES] + piece if to // LANES in parts else piece
            for j, v in parts.items():
                qrb[at : at + PAD, j * LANES : (j + 1) * LANES] = v
        else:
            sbb[at : at + PAD, own] = diag
    sub, lane = iota((8, LANES), 0), iota((8, LANES), 1)
    padded = (sub >= 6) & (sub == (lane & 7))
    tred = []
    for j in range(cols):
        m = dred[:, j * LANES : (j + 1) * LANES]
        m = jnp.where(padded, 1.0, m)
        for k in range(6):
            col = take(m, (lane & ~7) + k)
            row = jnp.broadcast_to(m[k : k + 1, :], (8, LANES))
            inv = 1.0 / jnp.broadcast_to(col[k : k + 1, :], (8, LANES))
            scaled = row * inv
            in_col, in_row = (lane & 7) == k, sub == k
            m = jnp.where(
                in_row,
                jnp.where(in_col, inv, scaled),
                jnp.where(in_col, -col * inv, m - col * scaled),
            )
        tred.append(m)
    dd = jnp.concatenate(
        [
            jnp.concatenate([jnp.where((lane + j * LANES) >> 3 == k, tred[j], 0.0) for j in range(cols)], axis=1)
            for k in range(half)
        ],
        axis=0,
    )
    q = qrb[...]
    t = dot(dd, q)
    r, c = iota((side, side), 0), iota((side, side), 1)
    sbb[...] = jnp.where((r == c) & ((r & 7) >= 6), 1.0, sbb[...] - dot(q, t, ((0,), (0,))))
    sweep(sbb, side)
    sinv = -sbb[...]
    ts = dot(t, sinv)
    def slot_of(pos, black):
        twice = 2 * pos
        odd = ((twice >> 2) ^ (twice >> 4)) & 1
        g = twice + ((1 - odd) if black else odd)
        return lax.rem(g + shift, n)

    rr, cc = iota((side, LANES), 0), iota((side, LANES), 1)
    sel = []
    for black in (False, True):
        slot = slot_of(rr >> 3, black)
        hit = jnp.zeros((side, LANES), jnp.bool_)
        for b, step in enumerate((0,) + STEPS):
            hit = hit | ((cc >> 3 == b) & (slot == lax.rem(sc[SLOT] + step + n, n)))
        sel.append(jnp.where(hit & ((rr & 7) == (cc & 7)), 1.0, 0.0).astype(F32))
    upper = dot(dd, sel[0]) + dot(ts, dot(t, sel[0], ((0,), (0,)))) - dot(ts, sel[1])
    lower = dot(sinv, sel[1]) - dot(ts, sel[0], ((0,), (0,)))
    pr, pc = iota((n * PAD, side), 0), iota((n * PAD, side), 1)
    out = None
    for black, x in ((False, upper), (True, lower)):
        onehot = jnp.where((slot_of(pc >> 3, black) == pr >> 3) & ((pc & 7) == (pr & 7)), 1.0, 0.0).astype(F32)
        v = dot(onehot, x)
        out = v if out is None else out + v
    return out


class Product:
    def __init__(self, b_hbm, b_vmem, sems):
        self.chunks = b_vmem.shape[0]
        rows = b_vmem.shape[1]
        self.copies = [
            pltpu.make_async_copy(b_hbm.at[0, pl.ds(k * rows, rows), :], b_vmem.at[k], sems.at[k]) for k in range(self.chunks)
        ]
        self.b = b_vmem
        for c in self.copies:
            c.start()

    def __call__(self, tiles, code, inv, acc, vec):
        blocks = len(tiles)
        moved = permute(lambda b: tiles[b], code, blocks)
        per = blocks // self.chunks
        for k in range(self.chunks):
            v = jnp.concatenate(moved[k * per : (k + 1) * per], axis=1)
            high = v.astype(jnp.bfloat16)
            low = (v - high.astype(F32)).astype(jnp.bfloat16)
            vec[k] = jnp.concatenate([high, low], axis=0)
        for k in range(self.chunks):
            self.copies[k].wait()
            part = dot(vec[k], self.b[k], precision=None)
            acc[...] = part if k == 0 else acc[...] + part
        return permute(lambda b: acc[0:8, b * LANES : (b + 1) * LANES] + acc[8:16, b * LANES : (b + 1) * LANES], inv, blocks)


def lanes_of(ref, b):
    return ref[:, b * LANES : (b + 1) * LANES]


def weigh(fc, f, t, x):
    return jnp.where(fc.shared(f, t), 0.5, jnp.where(fc.live(f, t), 1.0, 0.0)) * x


def total(tiles):
    acc = tiles[0]
    for x in tiles[1:]:
        acc = acc + x
    return jnp.sum(acc, axis=1, keepdims=True)


def coarse_of(n, recv, qloc):
    width = n * PAD
    rows = jnp.concatenate([recv[i] for i in range(n)], axis=0)
    dense = dot(rows, spread(n, width))
    goal = None
    both = None
    for i in range(n):
        x = dense[i * 8 : (i + 1) * 8, :]
        x = x if i == 0 else pltpu.roll(x, i * PAD, 1)
        goal = x if goal is None else goal + x
        both = recv[i] if both is None else both + recv[i]
    return dot(goal, qloc[...])[:, :EXTRA], both


def finish(n, fc, y, extra, c_ref, ybuf, tile_out):
    for b, v in enumerate(y):
        ybuf[:, b * LANES : (b + 1) * LANES] = v
    row = dot(ybuf[...], c_ref[...], ((1,), (1,)))
    tile = jnp.concatenate([row, jnp.zeros((8, LANES - EXTRA), F32)], axis=1)
    lane = iota((8, LANES), 1)
    for k, v in enumerate(extra):
        tile = jnp.where(lane == EXTRA + k, v, tile)
    for i in range(n):
        tile_out[i] = tile


def start_kernel(n, cap, faces, sc, b_hbm, recv, c_ref, rhs, code, inv, *refs):
    nm = len(pairings(n)[0])
    lam_out, t_out, q_out, tile_out = refs[:4]
    sends = refs[4 : 4 + nm]
    b_vmem, sems, acc, vec, dred, qrb, sbb = refs[4 + nm :]
    product = Product(b_hbm, b_vmem, sems)
    fc = Faces(sc, n, cap)
    blocks = cap * faces // LANES
    q_out[...] = invert(n, sc, recv, dred, qrb, sbb)
    goal = []
    for j in range(n * PAD // LANES):
        v = None
        for i in range(j * (LANES // PAD), (j + 1) * (LANES // PAD)):
            x = place(recv[i], EXTRA, (i * PAD) % LANES)
            v = x if v is None else v + x
        goal.append(v)
    z = dot(jnp.concatenate(goal, axis=1), q_out[...])[:, :EXTRA]
    lam_out[...] = dot(z, c_ref[...])
    y = product([lanes_of(lam_out, b) for b in range(blocks)], code, inv, acc, vec)
    t = [lanes_of(rhs, b) - y[b] for b in range(blocks)]
    fc.send(t, sends)
    finish(n, fc, t, [], c_ref, t_out, tile_out)


def assembled(fc, faces, c_ref, z, y_ref, far, buf):
    buf[...] = dot(z, c_ref[...])
    out = []
    for f in range(faces):
        for t in range(fc.per):
            b = f * fc.per + t
            v = lanes_of(y_ref, b) - fc.far(far, f, t)
            out.append(jnp.where(fc.live(f, t), v, 0.0) - lanes_of(buf, b))
    return out


def step_kernel(n, cap, faces, kind, sc, b_hbm, recv, c_ref, q_ref, code, inv, y_ref, *refs):
    refs = list(refs)
    nm = len(pairings(n)[0])
    pop = lambda k: [refs.pop(0) for _ in range(k)]
    far = pop(nm)
    state = pop({0: 0, 1: 2, 2: 5, 3: 5}[kind])
    fc = Faces(sc, n, cap)
    blocks = cap * faces // LANES
    if kind == 3:
        x_out, w_out, buf = refs
    else:
        w_out = pop(1)[0]
        x_out, p_out, s_out, k_out = pop(4) if kind else (None,) * 4
        y_out, tile_out = pop(2)
        sends = pop(nm)
        b_vmem, sems, acc, vec, buf = refs
        product = Product(b_hbm, b_vmem, sems)
    z, both = coarse_of(n, recv, q_ref)
    q = assembled(fc, faces, c_ref, z, y_ref, far, buf)
    if kind == 0:
        w, p, s = q, None, None
    else:
        rho, mu = both[:, EXTRA : EXTRA + 1], both[:, EXTRA + 1 : EXTRA + 2]
        w_old = [lanes_of(state[0], b) for b in range(blocks)]
        x_old = [lanes_of(state[1], b) for b in range(blocks)]
        if kind == 1:
            p, s, sigma = w_old, q, mu
        else:
            last = state[4][...]
            beta = rho / last[:, 0:1]
            cross = both[:, EXTRA + 2 : EXTRA + 3]
            sigma = mu + beta * cross + beta * beta * last[:, 1:2]
            p = [w_old[b] + beta * lanes_of(state[2], b) for b in range(blocks)]
            s = [q[b] + beta * lanes_of(state[3], b) for b in range(blocks)]
        alpha = rho / sigma
        w = [w_old[b] - alpha * s[b] for b in range(blocks)]
        x = [x_old[b] + alpha * p[b] for b in range(blocks)]
        if kind == 3:
            for out, v in ((x_out, x), (w_out, w)):
                for b, m in enumerate(permute(lambda b: v[b], code, blocks)):
                    out[0, :, b * LANES : (b + 1) * LANES] = m
            return
        lane = iota((8, LANES), 1)
        k_out[...] = jnp.where(lane == 0, rho, jnp.where(lane == 1, sigma, 0.0))
        for b in range(blocks):
            at = slice(b * LANES, (b + 1) * LANES)
            x_out[:, at], p_out[:, at], s_out[:, at] = x[b], p[b], s[b]
    for b in range(blocks):
        w_out[:, b * LANES : (b + 1) * LANES] = w[b]
    y = product(w, code, inv, acc, vec)
    fc.send(y, sends)
    w = [lanes_of(w_out, b) for b in range(blocks)]
    weighted = [weigh(fc, b // fc.per, b % fc.per, w[b]) for b in range(blocks)]
    extra = [total([weighted[b] * w[b] for b in range(blocks)]), total([w[b] * y[b] for b in range(blocks)])]
    if kind:
        extra.append(total([weighted[b] * lanes_of(s_out, b) + lanes_of(p_out, b) * y[b] for b in range(blocks)]))
    finish(n, fc, y, extra, c_ref, y_out, tile_out)


VMEM = pl.BlockSpec(memory_space=pltpu.VMEM)
SMEM = pl.BlockSpec(memory_space=pltpu.SMEM)
ANY = pl.BlockSpec(memory_space=pl.ANY)


def struct(*shape, dtype=F32):
    return jax.ShapeDtypeStruct(shape, dtype)


def per_device(
    dual_blocks, rigid_modes, dual_local, coarse_rhs, iface_sizes, neighbours, shared_counts, iface_map, owner
):
    n = lax.axis_size("dev")
    faces = neighbours.shape[1]
    nmax = iface_map.shape[1]
    cap = nmax // faces
    modes, loads = coarse_rhs.shape[1:]
    blocks = nmax // LANES
    pairs, _ = pairings(n)
    nm = len(pairs)
    params = pltpu.CompilerParams(vmem_limit_bytes=56 * 1024 * 1024)
    sc = jnp.concatenate(
        [
            lax.axis_index("dev").astype(jnp.int32)[None],
            owner[:1],
            iface_sizes,
            shared_counts[0],
            (neighbours[0] >= 0).astype(jnp.int32),
        ]
    )
    goal = jnp.zeros((8, LANES), F32).at[:loads, EXTRA : EXTRA + modes].set(coarse_rhs[0].T)
    vec = struct(8, nmax)
    face = [struct(8, cap)] * nm
    tiles = struct(n, 8, LANES)
    table = struct(blocks, LANES, dtype=jnp.int32)

    def call(kernel, name, in_specs, outs, scratch, *args):
        return pl.pallas_call(
            kernel,
            out_shape=outs,
            in_specs=in_specs,
            out_specs=[VMEM] * len(outs),
            scratch_shapes=scratch,
            compiler_params=params,
            name=name,
        )(*args)

    def exchange(parts):
        return [lax.ppermute(x, "dev", perm) for x, (_, _, perm) in zip(parts, pairs)]

    def everyone(x):
        return lax.all_to_all(x, "dev", 0, 0)

    modes_c, rhs_c, code, inv, *send = call(
        functools.partial(prepare_kernel, n, cap, faces),
        "prepare",
        [SMEM] + [VMEM] * 4,
        [vec, vec, table, table] + face,
        [pltpu.VMEM((8, nmax), F32)],
        sc,
        iface_map,
        iface_map.reshape(blocks, LANES),
        rigid_modes,
        dual_local,
    )
    far = exchange(send)
    c_mat, tile = call(
        functools.partial(row_kernel, n, cap, faces),
        "coarse_row",
        [SMEM] + [VMEM] * (2 + nm),
        [struct(EXTRA, nmax), tiles],
        [],
        sc,
        modes_c,
        goal,
        *far,
    )
    recv = everyone(tile)
    chunk = 256
    dense = [
        pltpu.VMEM((nmax // chunk, chunk, nmax), jnp.bfloat16),
        pltpu.SemaphoreType.DMA((nmax // chunk,)),
        pltpu.VMEM((16, nmax), F32),
        pltpu.VMEM((nmax // chunk, 16, chunk), jnp.bfloat16),
    ]
    side = n * PAD // 2
    x, y, q_mat, tile, *send = call(
        functools.partial(start_kernel, n, cap, faces),
        "start",
        [SMEM, ANY] + [VMEM] * 5,
        [vec, vec, struct(n * PAD, LANES), tiles] + face,
        dense + [pltpu.VMEM((8, side), F32), pltpu.VMEM((side, side), F32), pltpu.VMEM((side, side), F32)],
        sc,
        dual_blocks,
        recv,
        c_mat,
        rhs_c,
        code,
        inv,
    )
    state = []
    for kind in (0, 1, 2, 3):
        recv, far = everyone(tile), exchange(send)
        args = (sc, dual_blocks, recv, c_mat, q_mat, code, inv, y, *far, *state)
        specs = [SMEM, ANY] + [VMEM] * (len(args) - 2)
        body = functools.partial(step_kernel, n, cap, faces, kind)
        buf = [pltpu.VMEM((8, nmax), F32)]
        if kind == 3:
            return tuple(call(body, "last", specs, [struct(1, 8, nmax)] * 2, buf, *args))
        outs = [vec] + ([vec, vec, vec, struct(8, LANES)] if kind else []) + [vec, tiles] + face
        got = list(call(body, f"step{kind}", specs, outs, dense + buf, *args))
        w = got.pop(0)
        if kind:
            x, p, s, scal = got[:4]
            got = got[4:]
            state = [w, x, p, s, scal]
        else:
            state = [w, x]
        y, tile, send = got[0], got[1], got[2:]


def solution(mesh):
    return jax.shard_map(
        per_device,
        mesh=mesh,
        in_specs=(
            P("dev", None, None),
            P("dev", None, None),
            P("dev", None, None),
            P("dev", None, None),
            P("dev"),
            P("dev", None),
            P("dev", None),
            P("dev", None),
            P(),
        ),
        out_specs=(P("dev", None, None), P("dev", None, None)),
        check_vma=False,
    )
```

time: 954 us -> 174 us (0.18)
  blocking collectives: 429 us -> 11.5 us
  local copies, waits for them, and re-layouts: 283 us -> 7.39 us
  matrix products: 80.1 us -> 0 us
  Pallas kernels: 0 us -> 77.8 us
  other arithmetic: 72 us -> 2.63 us
  starting transfers between devices: 69.4 us -> 51.4 us
  waiting for transfers between devices: 7.84 us -> 21.4 us
    psum x9 -> x0, blocking collectives: 353 us -> none  [the longest x4 156 us: project(): coarse_all = lax.psum(placed, 'dev').reshape(devices * MODES, loads)]
    gather x38 -> x0, local copies, waits for them, and re-layouts: 213 us -> none  [the longest x20 139 us: spread_back(): return jnp.take(flattened, dof_codes, axis=1) * shared_float[None]]
    pallas_call x0 -> x7, Pallas kernels: none -> 77.8 us  [call(): pl.pallas_call(kernel, out_shape=outs, in_specs=in_specs, out_specs=[VMEM...]
    all_gather x2 -> x0, blocking collectives: 76 us -> none  [the longest x1 39.4 us: per_device(): lax.all_gather(block_row.reshape(MODES, devices * MODES), 'dev', axis=0,...]
    dot_general x20 -> x0, matrix products: 68.8 us -> none  [the longest x4 47.9 us: dual_apply(): lax.dot_general(vector.astype(jnp.bfloat16), dual_blocks[0], (((1,), (1,)...]
    another operation x20 -> x2, other arithmetic: 50.8 us -> 1.97 us  [the longest x7 28.7 us: per_device(): factor = jnp.linalg.cholesky(coarse_matrix)]
    ppermute x36 -> x25, starting transfers between devices: 69.4 us -> 39 us  [exchange(): lax.ppermute(x, 'dev', perm)]
    unnamed x203 -> x59, local copies, waits for them, and re-layouts: 27.1 us -> 4.72 us
  transfers between devices with their start and end apart: 36 -> 29, of which waited for: 2 -> 18; matrix products, arithmetic and copies ran while one was open for 4% -> 2% of each run, Pallas kernels for 0% -> 0%
where the time goes in v1:
time: 174 us
  Pallas kernels  77.8 us (45%)
  starting transfers between devices  51.4 us (30%)
  waiting for transfers between devices  21.4 us (12%)
  blocking collectives  11.5 us (7%)
  local copies, waits for them, and re-layouts  7.39 us (4%)
  other arithmetic  2.63 us (2%)
    pallas_call x7, Pallas kernels, call(): pl.pallas_call(kernel, out_shape=outs, in_specs=in_specs, out_specs=[VMEM...  77.8 us
    ppermute x25, starting transfers between devices, exchange(): lax.ppermute(x, 'dev', perm)  39 us
    ppermute x25, waiting for transfers between devices, exchange(): lax.ppermute(x, 'dev', perm)  21.4 us
    all_to_all x4, starting transfers between devices, everyone(): return lax.all_to_all(x, 'dev', 0, 0)  12.4 us
    all_to_all x1, blocking collectives, everyone(): return lax.all_to_all(x, 'dev', 0, 0)  11.5 us
    unnamed x59, local copies, waits for them, and re-layouts  4.72 us
  transfers between devices with their start and end apart: 29, of which 18 were waited for; matrix products, arithmetic and copies ran while one was open for 2% of the time, Pallas kernels for 0%

profile of v1, /device:TPU:0, one launch (start us, length us, event | category | flops | bytes accessed | tf_op | source)
XLA Modules:
  0.0 173.7 jit_solution(5025473436510335867)
XLA Ops:
  1.9 1.5 copy.11.modes
  3.5 1.9 %concatenate.5.sc = s32[15]{0:T(128)} concatenate(s32[1]{0:T(128)} %bitcast, s32[1]{0:T(128)} %bitcast.11, s32[1]{0:T(128)S(6)} %copy.17, s32[6]{0:T(128)} %bitcast.12, s32[6]{0:T(128)S(1)} %fusion.1), dimensions={0} | concatenate | bytes 120 | tf_op jit(solution)/shard_map/concatenate | solution.py:483
  5.4 3.5 %prepare.1 = (f32[8,3072]{1,0:T(8,128)}, f32[8,3072]{1,0:T(8,128)}, s32[24,128]{1,0:T(8,128)}, s32[24,128]{1,0:T(8,128)}, f32[8,512]{1,0:T(8,128)}, /*index=5*/f...) custom-call(s32[15]{0:T(128)} %concatenate.5.sc, s32[1,3072]{1,0:T(1,128)} %map_row.1, ...), custom_call_target="tpu_custom_call" | custom-call | tf_op jit(solution)/shard_map/prepare/pallas_call | solution.py:499
  9.4 6.6 %collective-permute-start.1 = (f32[8,512]{1,0:T(8,128)}, f32[8,512]{1,0:T(8,128)S(1)}, u32[]{:S(2)}, u32[]{:S(2)}) collective-permute-start(f32[8,512]{1,0:T(8,128)} %get-tuple-element.68), channel_id=1, source_target_pairs={{0,31},{1,2},{3,4},{5,6},{7,8},{9,10},{11,12},{13,14},{15,16},{17,... | collective-permute-start | bytes 49160 | tf_op jit(solution)/shard_map/ppermute | solution.py:510
  16.0 1.9 %collective-permute-start.3 = (f32[8,512]{1,0:T(8,128)}, f32[8,512]{1,0:T(8,128)S(1)}, u32[]{:S(2)}, u32[]{:S(2)}) collective-permute-start(f32[8,512]{1,0:T(8,128)} %get-tuple-element.70), channel_id=1, source_target_pairs={{0,28},{1,29},{2,30},{3,31},{4,8},{5,9},{6,10},{7,11},{12,16},{13,... | collective-permute-start | bytes 49160 | tf_op jit(solution)/shard_map/ppermute | solution.py:510
  18.5 1.3 fusion
  20.6 2.0 %collective-permute-done.3.refs_3_ = f32[8,512]{1,0:T(8,128)S(1)} collective-permute-done((f32[8,512]{1,0:T(8,128)}, f32[8,512]{1,0:T(8,128)S(1)}, u32[]{:S(2)}, u32[]{:S(2)}) %collective-permute-start.3) | collective-permute-done | bytes 16416 | tf_op jit(solution)/shard_map/ppermute | solution.py:510
  23.3 2.4 %coarse_row.1 = (f32[64,3072]{1,0:T(8,128)}, f32[32,8,128]{2,1,0:T(8,128)}) custom-call(s32[15]{0:T(128)} %concatenate.5.sc, f32[8,3072]{1,0:T(8,128)} %get-tuple-element.66.modes, f32[8,128]{1,0:T(8,128)} %scatter.4.goal, f32[8,512]{1,0:T(8,128)} %copy-done.14, f32[8,512]{1,0:T(8,128)} %copy-done.15, f32[8,512]{1,0:T(8,128)} %copy-done.16, ...), custom_call_target="tpu_custom_call" | custom-call | tf_op jit(solution)/shard_map/coarse_row/pallas_call | solution.py:499
  25.7 11.5 %all_to_all.25.recv = f32[32,8,128]{2,1,0:T(8,128)} all-to-all(f32[32,8,128]{2,1,0:T(8,128)} %get-tuple-element.72), channel_id=1, replica_groups=mesh['dev'=32] {'dev'}, dimensions={0} | all-to-all | bytes 262144 | tf_op jit(solution)/shard_map/all_to_all | solution.py:513
  37.2 33.4 %start.1 = (f32[8,3072]{1,0:T(8,128)}, f32[8,3072]{1,0:T(8,128)}, f32[256,128]{1,0:T(8,128)}, f32[32,8,128]{2,1,0:T(8,128)}, f32[8,512]{1,0:T(8,128)}, /*index=5...) custom-call(s32[15]{0:T(128)} %concatenate.5.sc, bf16[1,3072,3072]{2,1,0:T(8,128)(2,1)} %b_hbm.9, ...), custom_call_target="tpu_custom_call" | custom-call | tf_op jit(solution)/shard_map/start/pallas_call | solution.py:499
  70.6 2.8 %all-to-all-start.1 = ((f32[32,8,128]{2,1,0:T(8,128)}), f32[32,8,128]{2,1,0:T(8,128)S(1)}, u32[]{:S(2)}, u32[]{:S(2)}) async-start(f32[32,8,128]{2,1,0:T(8,128)} %get-tuple-element.77), calls=%async_computation.1 | async-start | bytes 262144 | tf_op jit(solution)/shard_map/all_to_all | solution.py:513
  73.5 5.4 %collective-permute-start.6 = (f32[8,512]{1,0:T(8,128)}, f32[8,512]{1,0:T(8,128)S(1)}, u32[]{:S(2)}, u32[]{:S(2)}) collective-permute-start(f32[8,512]{1,0:T(8,128)} %get-tuple-element.81), channel_id=1, source_target_pairs={{0,31},{1,2},{3,4},{5,6},{7,8},{9,10},{11,12},{13,14},{15,16},{17,... | collective-permute-start | bytes 49160 | tf_op jit(solution)/shard_map/ppermute | solution.py:510
  78.9 2.0 %collective-permute-start.8 = (f32[8,512]{1,0:T(8,128)}, f32[8,512]{1,0:T(8,128)S(1)}, u32[]{:S(2)}, u32[]{:S(2)}) collective-permute-start(f32[8,512]{1,0:T(8,128)} %get-tuple-element.83), channel_id=1, source_target_pairs={{0,28},{1,29},{2,30},{3,31},{4,8},{5,9},{6,10},{7,11},{12,16},{13,... | collective-permute-start | bytes 49160 | tf_op jit(solution)/shard_map/ppermute | solution.py:510
  81.7 1.2 collective-permute-done.7.refs_2_
  82.8 2.7 %collective-permute-done.8.refs_3_ = f32[8,512]{1,0:T(8,128)S(1)} collective-permute-done((f32[8,512]{1,0:T(8,128)}, f32[8,512]{1,0:T(8,128)S(1)}, u32[]{:S(2)}, u32[]{:S(2)}) %collective-permute-start.8) | collective-permute-done | bytes 16416 | tf_op jit(solution)/shard_map/ppermute | solution.py:510
  86.4 11.4 %step0.1 = (f32[8,3072]{1,0:T(8,128)}, f32[8,3072]{1,0:T(8,128)}, f32[32,8,128]{2,1,0:T(8,128)}, f32[8,512]{1,0:T(8,128)}, f32[8,512]{1,0:T(8,128)}, /*index=5*/...) custom-call(s32[15]{0:T(128)} %concatenate.5.sc, bf16[1,3072,3072]{2,1,0:T(8,128)(2,1)} %b_hbm.9, ...), custom_call_target="tpu_custom_call" | custom-call | tf_op jit(solution)/shard_map/step0/pallas_call | solution.py:499
  97.7 3.1 %all-to-all-start.2 = ((f32[32,8,128]{2,1,0:T(8,128)}), f32[32,8,128]{2,1,0:T(8,128)S(1)}, u32[]{:S(2)}, u32[]{:S(2)}) async-start(f32[32,8,128]{2,1,0:T(8,128)} %get-tuple-element.85), calls=%async_computation.2 | async-start | bytes 262144 | tf_op jit(solution)/shard_map/all_to_all | solution.py:513
  101.2 5.3 %collective-permute-start.11 = (f32[8,512]{1,0:T(8,128)}, f32[8,512]{1,0:T(8,128)S(1)}, u32[]{:S(2)}, u32[]{:S(2)}) collective-permute-start(f32[8,512]{1,0:T(8,128)} %get-tuple-element.88), channel_id=1, source_target_pairs={{0,31},{1,2},{3,4},{5,6},{7,8},{9,10},{11,12},{13,14},{15,16},{17,... | collective-permute-start | bytes 49160 | tf_op jit(solution)/shard_map/ppermute | solution.py:510
  106.5 2.0 %collective-permute-start.13 = (f32[8,512]{1,0:T(8,128)}, f32[8,512]{1,0:T(8,128)S(1)}, u32[]{:S(2)}, u32[]{:S(2)}) collective-permute-start(f32[8,512]{1,0:T(8,128)} %get-tuple-element.90), channel_id=1, source_target_pairs={{0,28},{1,29},{2,30},{3,31},{4,8},{5,9},{6,10},{7,11},{12,16},{13,... | collective-permute-start | bytes 49160 | tf_op jit(solution)/shard_map/ppermute | solution.py:510
  110.5 2.7 %collective-permute-done.13.refs_3_ = f32[8,512]{1,0:T(8,128)S(1)} collective-permute-done((f32[8,512]{1,0:T(8,128)}, f32[8,512]{1,0:T(8,128)S(1)}, u32[]{:S(2)}, u32[]{:S(2)}) %collective-permute-start.13) | collective-permute-done | bytes 16416 | tf_op jit(solution)/shard_map/ppermute | solution.py:510
  114.0 11.4 %step1.1 = (f32[8,3072]{1,0:T(8,128)}, f32[8,3072]{1,0:T(8,128)}, f32[8,3072]{1,0:T(8,128)}, f32[8,3072]{1,0:T(8,128)}, f32[8,128]{1,0:T(8,128)}, /*index=5*/f32...) custom-call(s32[15]{0:T(128)} %concatenate.5.sc, ...), custom_call_target="tpu_custom_call" | custom-call | tf_op jit(solution)/shard_map/step1/pallas_call | solution.py:499
  125.4 3.4 %all-to-all-start.3 = ((f32[32,8,128]{2,1,0:T(8,128)}), f32[32,8,128]{2,1,0:T(8,128)S(1)}, u32[]{:S(2)}, u32[]{:S(2)}) async-start(f32[32,8,128]{2,1,0:T(8,128)} %get-tuple-element.94), calls=%async_computation.3 | async-start | bytes 262144 | tf_op jit(solution)/shard_map/all_to_all | solution.py:513
  128.9 5.3 %collective-permute-start.16 = (f32[8,512]{1,0:T(8,128)}, f32[8,512]{1,0:T(8,128)S(1)}, u32[]{:S(2)}, u32[]{:S(2)}) collective-permute-start(f32[8,512]{1,0:T(8,128)} %get-tuple-element.97), channel_id=1, source_target_pairs={{0,31},{1,2},{3,4},{5,6},{7,8},{9,10},{11,12},{13,14},{15,16},{17,... | collective-permute-start | bytes 49160 | tf_op jit(solution)/shard_map/ppermute | solution.py:510
  134.2 2.0 %collective-permute-start.18 = (f32[8,512]{1,0:T(8,128)}, f32[8,512]{1,0:T(8,128)S(1)}, u32[]{:S(2)}, u32[]{:S(2)}) collective-permute-start(f32[8,512]{1,0:T(8,128)} %get-tuple-element.99), channel_id=1, source_target_pairs={{0,28},{1,29},{2,30},{3,31},{4,8},{5,9},{6,10},{7,11},{12,16},{13,... | collective-permute-start | bytes 49160 | tf_op jit(solution)/shard_map/ppermute | solution.py:510
  137.0 1.2 collective-permute-done.17.refs_2_
  138.2 2.7 %collective-permute-done.18.refs_3_ = f32[8,512]{1,0:T(8,128)S(1)} collective-permute-done((f32[8,512]{1,0:T(8,128)}, f32[8,512]{1,0:T(8,128)S(1)}, u32[]{:S(2)}, u32[]{:S(2)}) %collective-permute-start.18) | collective-permute-done | bytes 16416 | tf_op jit(solution)/shard_map/ppermute | solution.py:510
  141.7 11.1 %step2.1 = (f32[8,3072]{1,0:T(8,128)}, f32[8,3072]{1,0:T(8,128)}, f32[8,3072]{1,0:T(8,128)}, f32[8,3072]{1,0:T(8,128)}, f32[8,128]{1,0:T(8,128)}, /*index=5*/f32...) custom-call(s32[15]{0:T(128)} %concatenate.5.sc, ...), custom_call_target="tpu_custom_call" | custom-call | tf_op jit(solution)/shard_map/step2/pallas_call | solution.py:499
  152.8 3.1 %all-to-all-start.4 = ((f32[32,8,128]{2,1,0:T(8,128)}), f32[32,8,128]{2,1,0:T(8,128)S(1)}, u32[]{:S(2)}, u32[]{:S(2)}) async-start(f32[32,8,128]{2,1,0:T(8,128)} %get-tuple-element.106), calls=%async_computation.4 | async-start | bytes 262144 | tf_op jit(solution)/shard_map/all_to_all | solution.py:513
  156.2 5.3 %collective-permute-start.21 = (f32[8,512]{1,0:T(8,128)}, f32[8,512]{1,0:T(8,128)S(1)}, u32[]{:S(2)}, u32[]{:S(2)}) collective-permute-start(f32[8,512]{1,0:T(8,128)} %get-tuple-element.109), channel_id=1, source_target_pairs={{0,31},{1,2},{3,4},{5,6},{7,8},{9,10},{11,12},{13,14},{15,16},{17,... | collective-permute-start | bytes 49160 | tf_op jit(solution)/shard_map/ppermute | solution.py:510
  161.6 2.0 %collective-permute-start.23 = (f32[8,512]{1,0:T(8,128)}, f32[8,512]{1,0:T(8,128)S(1)}, u32[]{:S(2)}, u32[]{:S(2)}) collective-permute-start(f32[8,512]{1,0:T(8,128)} %get-tuple-element.111), channel_id=1, source_target_pairs={{0,28},{1,29},{2,30},{3,31},{4,8},{5,9},{6,10},{7,11},{12,16},{13,... | collective-permute-start | bytes 49160 | tf_op jit(solution)/shard_map/ppermute | solution.py:510
  165.5 2.7 %collective-permute-done.23.refs_3_ = f32[8,512]{1,0:T(8,128)S(1)} collective-permute-done((f32[8,512]{1,0:T(8,128)}, f32[8,512]{1,0:T(8,128)S(1)}, u32[]{:S(2)}, u32[]{:S(2)}) %collective-permute-start.23) | collective-permute-done | bytes 16416 | tf_op jit(solution)/shard_map/ppermute | solution.py:510
  169.0 4.7 %last.1 = (f32[1,8,3072]{2,1,0:T(8,128)}, f32[1,8,3072]{2,1,0:T(8,128)}) custom-call(s32[15]{0:T(128)} %concatenate.5.sc, bf16[1,3072,3072]{2,1,0:T(8,128)(2,1)} %b_hbm.9, f32[32,8,128]{2,1,0:T(8,128)} %copy-done.2, f32[64,3072]{1,0:T(8,128)} %get-tuple-element.73.c_ref, f32[256,128]{1,0:T(8,128)} %get-tuple-element.78.q_ref, ...), custom_call_target="tpu_custom_call" | custom-call | tf_op jit(solution)/shard_map/last/pallas_call | solution.py:499
  (99 shorter events, 12.9 us)
Async XLA Ops:
  8.9 11.7 %collective-permute-start = (f32[8,512]{1,0:T(8,128)}, f32[8,512]{1,0:T(8,128)S(1)}, u32[]{:S(2)}, u32[]{:S(2)}) collective-permute-start(f32[8,512]{1,0:T(8,128)} %get-tuple-element.67), channel_id=1, source_target_pairs={{0,1},{2,3},{4,5},{6,7},{8,9},{10,11},{12,13},{14,15},{16,17},{18,... | collective-permute-start | bytes 49160 | tf_op jit(solution)/shard_map/ppermute | solution.py:510
  9.4 11.2 %collective-permute-start.1 = (f32[8,512]{1,0:T(8,128)}, f32[8,512]{1,0:T(8,128)S(1)}, u32[]{:S(2)}, u32[]{:S(2)}) collective-permute-start(f32[8,512]{1,0:T(8,128)} %get-tuple-element.68), channel_id=1, source_target_pairs={{0,31},{1,2},{3,4},{5,6},{7,8},{9,10},{11,12},{13,14},{15,16},{17,... | collective-permute-start | bytes 49160 | tf_op jit(solution)/shard_map/ppermute | solution.py:510
  15.9 4.7 %collective-permute-start.2 = (f32[8,512]{1,0:T(8,128)}, f32[8,512]{1,0:T(8,128)S(1)}, u32[]{:S(2)}, u32[]{:S(2)}) collective-permute-start(f32[8,512]{1,0:T(8,128)} %get-tuple-element.69), channel_id=1, source_target_pairs={{0,4},{1,5},{2,6},{3,7},{8,12},{9,13},{10,14},{11,15},{16,20},{17,... | collective-permute-start | bytes 49160 | tf_op jit(solution)/shard_map/ppermute | solution.py:510
  16.0 6.6 %collective-permute-start.3 = (f32[8,512]{1,0:T(8,128)}, f32[8,512]{1,0:T(8,128)S(1)}, u32[]{:S(2)}, u32[]{:S(2)}) collective-permute-start(f32[8,512]{1,0:T(8,128)} %get-tuple-element.70), channel_id=1, source_target_pairs={{0,28},{1,29},{2,30},{3,31},{4,8},{5,9},{6,10},{7,11},{12,16},{13,... | collective-permute-start | bytes 49160 | tf_op jit(solution)/shard_map/ppermute | solution.py:510
  17.9 4.8 %collective-permute-start.4 = (f32[8,512]{1,0:T(8,128)}, f32[8,512]{1,0:T(8,128)S(1)}, u32[]{:S(2)}, u32[]{:S(2)}) collective-permute-start(f32[8,512]{1,0:T(8,128)} %get-tuple-element.71), channel_id=1, source_target_pairs={{0,16},{1,17},{2,18},{3,19},{4,20},{5,21},{6,22},{7,23},{8,24},{9,... | collective-permute-start | bytes 49160 | tf_op jit(solution)/shard_map/ppermute | solution.py:510
  70.6 15.1 %all-to-all-start.1 = ((f32[32,8,128]{2,1,0:T(8,128)}), f32[32,8,128]{2,1,0:T(8,128)S(1)}, u32[]{:S(2)}, u32[]{:S(2)}) async-start(f32[32,8,128]{2,1,0:T(8,128)} %get-tuple-element.77), calls=%async_computation.1 | async-start | bytes 262144 | tf_op jit(solution)/shard_map/all_to_all | solution.py:513
  73.4 7.4 %collective-permute-start.5 = (f32[8,512]{1,0:T(8,128)}, f32[8,512]{1,0:T(8,128)S(1)}, u32[]{:S(2)}, u32[]{:S(2)}) collective-permute-start(f32[8,512]{1,0:T(8,128)} %get-tuple-element.80), channel_id=1, source_target_pairs={{0,1},{2,3},{4,5},{6,7},{8,9},{10,11},{12,13},{14,15},{16,17},{18,... | collective-permute-start | bytes 49160 | tf_op jit(solution)/shard_map/ppermute | solution.py:510
  73.5 8.2 %collective-permute-start.6 = (f32[8,512]{1,0:T(8,128)}, f32[8,512]{1,0:T(8,128)S(1)}, u32[]{:S(2)}, u32[]{:S(2)}) collective-permute-start(f32[8,512]{1,0:T(8,128)} %get-tuple-element.81), channel_id=1, source_target_pairs={{0,31},{1,2},{3,4},{5,6},{7,8},{9,10},{11,12},{13,14},{15,16},{17,... | collective-permute-start | bytes 49160 | tf_op jit(solution)/shard_map/ppermute | solution.py:510
  78.9 3.9 %collective-permute-start.7 = (f32[8,512]{1,0:T(8,128)}, f32[8,512]{1,0:T(8,128)S(1)}, u32[]{:S(2)}, u32[]{:S(2)}) collective-permute-start(f32[8,512]{1,0:T(8,128)} %get-tuple-element.82), channel_id=1, source_target_pairs={{0,4},{1,5},{2,6},{3,7},{8,12},{9,13},{10,14},{11,15},{16,20},{17,... | collective-permute-start | bytes 49160 | tf_op jit(solution)/shard_map/ppermute | solution.py:510
  78.9 6.6 %collective-permute-start.8 = (f32[8,512]{1,0:T(8,128)}, f32[8,512]{1,0:T(8,128)S(1)}, u32[]{:S(2)}, u32[]{:S(2)}) collective-permute-start(f32[8,512]{1,0:T(8,128)} %get-tuple-element.83), channel_id=1, source_target_pairs={{0,28},{1,29},{2,30},{3,31},{4,8},{5,9},{6,10},{7,11},{12,16},{13,... | collective-permute-start | bytes 49160 | tf_op jit(solution)/shard_map/ppermute | solution.py:510
  80.8 4.8 %collective-permute-start.9 = (f32[8,512]{1,0:T(8,128)}, f32[8,512]{1,0:T(8,128)S(1)}, u32[]{:S(2)}, u32[]{:S(2)}) collective-permute-start(f32[8,512]{1,0:T(8,128)} %get-tuple-element.84), channel_id=1, source_target_pairs={{0,16},{1,17},{2,18},{3,19},{4,20},{5,21},{6,22},{7,23},{8,24},{9,... | collective-permute-start | bytes 49160 | tf_op jit(solution)/shard_map/ppermute | solution.py:510
  80.9 4.9 %copy-start.22 = (f32[8,512]{1,0:T(8,128)}, f32[8,512]{1,0:T(8,128)S(1)}, u32[]{:S(2)}) copy-start(f32[8,512]{1,0:T(8,128)S(1)} %collective-permute-done.5.refs_0_) | copy-start | bytes 49156
  97.7 15.6 %all-to-all-start.2 = ((f32[32,8,128]{2,1,0:T(8,128)}), f32[32,8,128]{2,1,0:T(8,128)S(1)}, u32[]{:S(2)}, u32[]{:S(2)}) async-start(f32[32,8,128]{2,1,0:T(8,128)} %get-tuple-element.85), calls=%async_computation.2 | async-start | bytes 262144 | tf_op jit(solution)/shard_map/all_to_all | solution.py:513
  100.9 7.6 %collective-permute-start.10 = (f32[8,512]{1,0:T(8,128)}, f32[8,512]{1,0:T(8,128)S(1)}, u32[]{:S(2)}, u32[]{:S(2)}) collective-permute-start(f32[8,512]{1,0:T(8,128)} %get-tuple-element.87), channel_id=1, source_target_pairs={{0,1},{2,3},{4,5},{6,7},{8,9},{10,11},{12,13},{14,15},{16,17},{18,... | collective-permute-start | bytes 49160 | tf_op jit(solution)/shard_map/ppermute | solution.py:510
  101.2 8.1 %collective-permute-start.11 = (f32[8,512]{1,0:T(8,128)}, f32[8,512]{1,0:T(8,128)S(1)}, u32[]{:S(2)}, u32[]{:S(2)}) collective-permute-start(f32[8,512]{1,0:T(8,128)} %get-tuple-element.88), channel_id=1, source_target_pairs={{0,31},{1,2},{3,4},{5,6},{7,8},{9,10},{11,12},{13,14},{15,16},{17,... | collective-permute-start | bytes 49160 | tf_op jit(solution)/shard_map/ppermute | solution.py:510
  106.5 3.9 %collective-permute-start.12 = (f32[8,512]{1,0:T(8,128)}, f32[8,512]{1,0:T(8,128)S(1)}, u32[]{:S(2)}, u32[]{:S(2)}) collective-permute-start(f32[8,512]{1,0:T(8,128)} %get-tuple-element.89), channel_id=1, source_target_pairs={{0,4},{1,5},{2,6},{3,7},{8,12},{9,13},{10,14},{11,15},{16,20},{17,... | collective-permute-start | bytes 49160 | tf_op jit(solution)/shard_map/ppermute | solution.py:510
  106.5 6.6 %collective-permute-start.13 = (f32[8,512]{1,0:T(8,128)}, f32[8,512]{1,0:T(8,128)S(1)}, u32[]{:S(2)}, u32[]{:S(2)}) collective-permute-start(f32[8,512]{1,0:T(8,128)} %get-tuple-element.90), channel_id=1, source_target_pairs={{0,28},{1,29},{2,30},{3,31},{4,8},{5,9},{6,10},{7,11},{12,16},{13,... | collective-permute-start | bytes 49160 | tf_op jit(solution)/shard_map/ppermute | solution.py:510
  108.5 4.8 %collective-permute-start.14 = (f32[8,512]{1,0:T(8,128)}, f32[8,512]{1,0:T(8,128)S(1)}, u32[]{:S(2)}, u32[]{:S(2)}) collective-permute-start(f32[8,512]{1,0:T(8,128)} %get-tuple-element.91), channel_id=1, source_target_pairs={{0,16},{1,17},{2,18},{3,19},{4,20},{5,21},{6,22},{7,23},{8,24},{9,... | collective-permute-start | bytes 49160 | tf_op jit(solution)/shard_map/ppermute | solution.py:510
  108.5 4.9 %copy-start.19 = (f32[8,512]{1,0:T(8,128)}, f32[8,512]{1,0:T(8,128)S(1)}, u32[]{:S(2)}) copy-start(f32[8,512]{1,0:T(8,128)S(1)} %collective-permute-done.10.refs_0_) | copy-start | bytes 49156
  125.4 15.6 %all-to-all-start.3 = ((f32[32,8,128]{2,1,0:T(8,128)}), f32[32,8,128]{2,1,0:T(8,128)S(1)}, u32[]{:S(2)}, u32[]{:S(2)}) async-start(f32[32,8,128]{2,1,0:T(8,128)} %get-tuple-element.94), calls=%async_computation.3 | async-start | bytes 262144 | tf_op jit(solution)/shard_map/all_to_all | solution.py:513
  128.8 7.4 %collective-permute-start.15 = (f32[8,512]{1,0:T(8,128)}, f32[8,512]{1,0:T(8,128)S(1)}, u32[]{:S(2)}, u32[]{:S(2)}) collective-permute-start(f32[8,512]{1,0:T(8,128)} %get-tuple-element.96), channel_id=1, source_target_pairs={{0,1},{2,3},{4,5},{6,7},{8,9},{10,11},{12,13},{14,15},{16,17},{18,... | collective-permute-start | bytes 49160 | tf_op jit(solution)/shard_map/ppermute | solution.py:510
  128.9 8.1 %collective-permute-start.16 = (f32[8,512]{1,0:T(8,128)}, f32[8,512]{1,0:T(8,128)S(1)}, u32[]{:S(2)}, u32[]{:S(2)}) collective-permute-start(f32[8,512]{1,0:T(8,128)} %get-tuple-element.97), channel_id=1, source_target_pairs={{0,31},{1,2},{3,4},{5,6},{7,8},{9,10},{11,12},{13,14},{15,16},{17,... | collective-permute-start | bytes 49160 | tf_op jit(solution)/shard_map/ppermute | solution.py:510
  134.2 3.9 %collective-permute-start.17 = (f32[8,512]{1,0:T(8,128)}, f32[8,512]{1,0:T(8,128)S(1)}, u32[]{:S(2)}, u32[]{:S(2)}) collective-permute-start(f32[8,512]{1,0:T(8,128)} %get-tuple-element.98), channel_id=1, source_target_pairs={{0,4},{1,5},{2,6},{3,7},{8,12},{9,13},{10,14},{11,15},{16,20},{17,... | collective-permute-start | bytes 49160 | tf_op jit(solution)/shard_map/ppermute | solution.py:510
  134.2 6.6 %collective-permute-start.18 = (f32[8,512]{1,0:T(8,128)}, f32[8,512]{1,0:T(8,128)S(1)}, u32[]{:S(2)}, u32[]{:S(2)}) collective-permute-start(f32[8,512]{1,0:T(8,128)} %get-tuple-element.99), channel_id=1, source_target_pairs={{0,28},{1,29},{2,30},{3,31},{4,8},{5,9},{6,10},{7,11},{12,16},{13,... | collective-permute-start | bytes 49160 | tf_op jit(solution)/shard_map/ppermute | solution.py:510
  136.2 4.8 %collective-permute-start.19 = (f32[8,512]{1,0:T(8,128)}, f32[8,512]{1,0:T(8,128)S(1)}, u32[]{:S(2)}, u32[]{:S(2)}) collective-permute-start(f32[8,512]{1,0:T(8,128)} %get-tuple-element.100), channel_id=1, source_target_pairs={{0,16},{1,17},{2,18},{3,19},{4,20},{5,21},{6,22},{7,23},{8,24},{9,... | collective-permute-start | bytes 49160 | tf_op jit(solution)/shard_map/ppermute | solution.py:510
  136.2 4.9 %copy-start.4 = (f32[8,512]{1,0:T(8,128)}, f32[8,512]{1,0:T(8,128)S(1)}, u32[]{:S(2)}) copy-start(f32[8,512]{1,0:T(8,128)S(1)} %collective-permute-done.15.refs_0_) | copy-start | bytes 49156
  152.8 15.6 %all-to-all-start.4 = ((f32[32,8,128]{2,1,0:T(8,128)}), f32[32,8,128]{2,1,0:T(8,128)S(1)}, u32[]{:S(2)}, u32[]{:S(2)}) async-start(f32[32,8,128]{2,1,0:T(8,128)} %get-tuple-element.106), calls=%async_computation.4 | async-start | bytes 262144 | tf_op jit(solution)/shard_map/all_to_all | solution.py:513
  155.9 7.6 %collective-permute-start.20 = (f32[8,512]{1,0:T(8,128)}, f32[8,512]{1,0:T(8,128)S(1)}, u32[]{:S(2)}, u32[]{:S(2)}) collective-permute-start(f32[8,512]{1,0:T(8,128)} %get-tuple-element.108), channel_id=1, source_target_pairs={{0,1},{2,3},{4,5},{6,7},{8,9},{10,11},{12,13},{14,15},{16,17},{18,... | collective-permute-start | bytes 49160 | tf_op jit(solution)/shard_map/ppermute | solution.py:510
  156.2 8.1 %collective-permute-start.21 = (f32[8,512]{1,0:T(8,128)}, f32[8,512]{1,0:T(8,128)S(1)}, u32[]{:S(2)}, u32[]{:S(2)}) collective-permute-start(f32[8,512]{1,0:T(8,128)} %get-tuple-element.109), channel_id=1, source_target_pairs={{0,31},{1,2},{3,4},{5,6},{7,8},{9,10},{11,12},{13,14},{15,16},{17,... | collective-permute-start | bytes 49160 | tf_op jit(solution)/shard_map/ppermute | solution.py:510
  161.6 3.9 %collective-permute-start.22 = (f32[8,512]{1,0:T(8,128)}, f32[8,512]{1,0:T(8,128)S(1)}, u32[]{:S(2)}, u32[]{:S(2)}) collective-permute-start(f32[8,512]{1,0:T(8,128)} %get-tuple-element.110), channel_id=1, source_target_pairs={{0,4},{1,5},{2,6},{3,7},{8,12},{9,13},{10,14},{11,15},{16,20},{17,... | collective-permute-start | bytes 49160 | tf_op jit(solution)/shard_map/ppermute | solution.py:510
  161.6 6.6 %collective-permute-start.23 = (f32[8,512]{1,0:T(8,128)}, f32[8,512]{1,0:T(8,128)S(1)}, u32[]{:S(2)}, u32[]{:S(2)}) collective-permute-start(f32[8,512]{1,0:T(8,128)} %get-tuple-element.111), channel_id=1, source_target_pairs={{0,28},{1,29},{2,30},{3,31},{4,8},{5,9},{6,10},{7,11},{12,16},{13,... | collective-permute-start | bytes 49160 | tf_op jit(solution)/shard_map/ppermute | solution.py:510
  163.5 4.8 %collective-permute-start.24 = (f32[8,512]{1,0:T(8,128)}, f32[8,512]{1,0:T(8,128)S(1)}, u32[]{:S(2)}, u32[]{:S(2)}) collective-permute-start(f32[8,512]{1,0:T(8,128)} %get-tuple-element.112), channel_id=1, source_target_pairs={{0,16},{1,17},{2,18},{3,19},{4,20},{5,21},{6,22},{7,23},{8,24},{9,... | collective-permute-start | bytes 49160 | tf_op jit(solution)/shard_map/ppermute | solution.py:510
  (26 other events, 47.6 us)

commit v2 on v1

--- a/solution.py
+++ b/solution.py
@@ -55,10 +55,6 @@
     return out
 
 
-def tile_of(ref):
-    return lambda b: ref[:, b * LANES : (b + 1) * LANES]
-
-
 class Faces:
     def __init__(self, sc, n, cap):
         self.sc, self.n, self.cap = sc, n, cap
@@ -101,10 +97,16 @@
     return jnp.where(hit, 1.0, 0.0).astype(F32)
 
 
-def prepare_kernel(n, cap, faces, sc, map_row, map_tile, modes, rhs, *refs):
+def prepare_kernel(n, cap, faces, owner, sizes, counts, links, map_row, map_tile, modes, rhs, sc, *refs):
     nm = len(pairings(n)[0])
     modes_out, rhs_out, code_out, inv_out = refs[:4]
-    sends, scratch = refs[4 : 4 + nm], refs[4 + nm]
+    sends = refs[4 : 4 + nm]
+    sc[SLOT] = lax.axis_index("dev").astype(jnp.int32)
+    sc[SHIFT] = owner[0]
+    sc[SIZE] = sizes[0]
+    for f in range(faces):
+        sc[COUNT + f] = counts[0, f]
+        sc[LINK + f] = (links[0, f] >= 0).astype(jnp.int32)
     nmax = cap * faces
     blocks = nmax // LANES
     size = sc[SIZE]
@@ -128,9 +130,11 @@
     inv_out[...] = inv[:blocks]
     tile_j = iota((blocks, LANES), 0) * LANES + iota((blocks, LANES), 1)
     code_out[...] = jnp.where(tile_j < size, map_tile[...], -1)
-    scratch[...] = jnp.zeros_like(scratch)
-    scratch[: modes.shape[1], :] = modes[0]
-    moved = permute(tile_of(scratch), inv_out, blocks)
+    count = modes.shape[0] // blocks
+    rest = jnp.zeros((8 - count, LANES), F32)
+    moved = permute(
+        lambda b: jnp.concatenate([modes[pl.ds(b, count, blocks), :], rest], axis=0), inv_out, blocks
+    )
     for b, v in enumerate(moved):
         modes_out[:, b * LANES : (b + 1) * LANES] = v
     Faces(sc, n, cap).send(moved, sends)
@@ -149,7 +153,9 @@
             at = f * cap + t * LANES
             c_out[PAD * (1 + f) : PAD * (2 + f), at : at + LANES] = -fc.far(ins, f, t)
     row = dot(modes[...], c_out[...], ((1,), (1,)))
-    tile = jnp.concatenate([row, jnp.zeros((8, LANES - EXTRA), F32)], axis=1) + goal[...]
+    count = goal.shape[0]
+    onehot = jnp.where(iota((count, LANES), 1) == iota((count, LANES), 0) + EXTRA, 1.0, 0.0).astype(F32)
+    tile = jnp.concatenate([row, jnp.zeros((8, LANES - EXTRA), F32)], axis=1) + dot(goal[...], onehot, ((0,), (0,)))
     for i in range(n):
         tile_out[i] = tile
 
@@ -160,11 +166,11 @@
 
     def step(b, carry):
         at = pl.multiple_of(b * PAD, PAD)
-        column = pl.multiple_of((at // LANES) * LANES, LANES)
+        column = 0 if cols == 1 else pl.multiple_of((at // LANES) * LANES, LANES)
         lane0 = at - column
         sub, lane = iota((8, LANES), 0), iota((8, LANES), 1)
         rows = [ref[pl.ds(at, PAD), j * LANES : (j + 1) * LANES] for j in range(cols)]
-        pivot = ref[pl.ds(at, PAD), pl.ds(column, LANES)]
+        pivot = rows[0] if cols == 1 else ref[pl.ds(at, PAD), pl.ds(column, LANES)]
         g = [take(pivot, jnp.full((8, LANES), 0, jnp.int32) + (lane0 + c)) for c in range(reals)]
         for k in range(reals):
             top = [jnp.broadcast_to(g[c][k : k + 1, :], (8, LANES)) for c in range(reals)]
@@ -189,15 +195,25 @@
                 minus = jnp.where(lane + j * LANES == at + c, -g[c], minus)
             w.append((minus, here))
         wb = [[jnp.broadcast_to(w[j][0][c : c + 1, :], (8, LANES)) for c in range(reals)] for j in range(cols)]
-        for i in range(side // PAD):
-            r = slice(i * PAD, (i + 1) * PAD)
-            src = ref[r, pl.ds(column, LANES)]
-            splat = [take(src, jnp.full((8, LANES), 0, jnp.int32) + (lane0 + c)) for c in range(reals)]
-            for j in range(cols):
-                x = jnp.where(w[j][1], 0.0, ref[r, j * LANES : (j + 1) * LANES])
+        if cols == 1:
+            lanes = [jnp.full((8, LANES), 0, jnp.int32) + (lane0 + c) for c in range(reals)]
+            olds = [ref[i * PAD : (i + 1) * PAD, :] for i in range(side // PAD)]
+            splats = [[take(x, i) for i in lanes] for x in olds]
+            for i, x in enumerate(olds):
+                x = jnp.where(w[0][1], 0.0, x)
                 for c in range(reals):
-                    x = x - splat[c] * wb[j][c]
-                ref[r, j * LANES : (j + 1) * LANES] = x
+                    x = x - splats[i][c] * wb[0][c]
+                ref[i * PAD : (i + 1) * PAD, :] = x
+        else:
+            for i in range(side // PAD):
+                r = slice(i * PAD, (i + 1) * PAD)
+                src = ref[r, pl.ds(column, LANES)]
+                splat = [take(src, jnp.full((8, LANES), 0, jnp.int32) + (lane0 + c)) for c in range(reals)]
+                for j in range(cols):
+                    x = jnp.where(w[j][1], 0.0, ref[r, j * LANES : (j + 1) * LANES])
+                    for c in range(reals):
+                        x = x - splat[c] * wb[j][c]
+                    ref[r, j * LANES : (j + 1) * LANES] = x
         for j in range(cols):
             ref[pl.ds(at, PAD), j * LANES : (j + 1) * LANES] = jnp.where(sub < reals, w[j][0], rows[j])
         return carry
@@ -298,17 +314,20 @@
 
 
 class Product:
-    def __init__(self, b_hbm, b_vmem, sems):
-        self.chunks = b_vmem.shape[0]
-        rows = b_vmem.shape[1]
-        self.copies = [
-            pltpu.make_async_copy(b_hbm.at[0, pl.ds(k * rows, rows), :], b_vmem.at[k], sems.at[k]) for k in range(self.chunks)
-        ]
-        self.b = b_vmem
-        for c in self.copies:
-            c.start()
-
-    def __call__(self, tiles, code, inv, acc, vec):
+    def __init__(self, b_hbm, b_vmem, sems, acc, vec):
+        self.b, self.acc, self.vec = b_vmem, acc, vec
+        self.chunks, rows = b_vmem.shape[:2]
+        self.copy = lambda k: pltpu.make_async_copy(b_hbm.at[0, pl.ds(k * rows, rows), :], b_vmem.at[k], sems.at[k])
+
+    def start(self):
+        def one(k, carry):
+            self.copy(k).start()
+            return carry
+
+        lax.fori_loop(0, self.chunks, one, 0)
+
+    def __call__(self, tiles, code, inv):
+        acc, vec = self.acc, self.vec
         blocks = len(tiles)
         moved = permute(lambda b: tiles[b], code, blocks)
         per = blocks // self.chunks
@@ -318,7 +337,7 @@
             low = (v - high.astype(F32)).astype(jnp.bfloat16)
             vec[k] = jnp.concatenate([high, low], axis=0)
         for k in range(self.chunks):
-            self.copies[k].wait()
+            self.copy(k).wait()
             part = dot(vec[k], self.b[k], precision=None)
             acc[...] = part if k == 0 else acc[...] + part
         return permute(lambda b: acc[0:8, b * LANES : (b + 1) * LANES] + acc[8:16, b * LANES : (b + 1) * LANES], inv, blocks)
@@ -365,12 +384,11 @@
         tile_out[i] = tile
 
 
-def start_kernel(n, cap, faces, sc, b_hbm, recv, c_ref, rhs, code, inv, *refs):
+def start_kernel(n, cap, faces, product, sc, recv, c_ref, rhs, code, inv, *refs):
     nm = len(pairings(n)[0])
     lam_out, t_out, q_out, tile_out = refs[:4]
     sends = refs[4 : 4 + nm]
-    b_vmem, sems, acc, vec, dred, qrb, sbb = refs[4 + nm :]
-    product = Product(b_hbm, b_vmem, sems)
+    dred, qrb, sbb = refs[4 + nm :]
     fc = Faces(sc, n, cap)
     blocks = cap * faces // LANES
     q_out[...] = invert(n, sc, recv, dred, qrb, sbb)
@@ -383,7 +401,7 @@
         goal.append(v)
     z = dot(jnp.concatenate(goal, axis=1), q_out[...])[:, :EXTRA]
     lam_out[...] = dot(z, c_ref[...])
-    y = product([lanes_of(lam_out, b) for b in range(blocks)], code, inv, acc, vec)
+    y = product([lanes_of(lam_out, b) for b in range(blocks)], code, inv)
     t = [lanes_of(rhs, b) - y[b] for b in range(blocks)]
     fc.send(t, sends)
     finish(n, fc, t, [], c_ref, t_out, tile_out)
@@ -400,7 +418,7 @@
     return out
 
 
-def step_kernel(n, cap, faces, kind, sc, b_hbm, recv, c_ref, q_ref, code, inv, y_ref, *refs):
+def step_kernel(n, cap, faces, kind, product, sc, recv, c_ref, q_ref, code, inv, y_ref, *refs):
     refs = list(refs)
     nm = len(pairings(n)[0])
     pop = lambda k: [refs.pop(0) for _ in range(k)]
@@ -415,8 +433,7 @@
         x_out, p_out, s_out, k_out = pop(4) if kind else (None,) * 4
         y_out, tile_out = pop(2)
         sends = pop(nm)
-        b_vmem, sems, acc, vec, buf = refs
-        product = Product(b_hbm, b_vmem, sems)
+        (buf,) = refs
     z, both = coarse_of(n, recv, q_ref)
     q = assembled(fc, faces, c_ref, z, y_ref, far, buf)
     if kind == 0:
@@ -449,7 +466,7 @@
             x_out[:, at], p_out[:, at], s_out[:, at] = x[b], p[b], s[b]
     for b in range(blocks):
         w_out[:, b * LANES : (b + 1) * LANES] = w[b]
-    y = product(w, code, inv, acc, vec)
+    y = product(w, code, inv)
     fc.send(y, sends)
     w = [lanes_of(w_out, b) for b in range(blocks)]
     weighted = [weigh(fc, b // fc.per, b % fc.per, w[b]) for b in range(blocks)]
@@ -480,31 +497,47 @@
     pairs, _ = pairings(n)
     nm = len(pairs)
     params = pltpu.CompilerParams(vmem_limit_bytes=56 * 1024 * 1024)
-    sc = jnp.concatenate(
-        [
-            lax.axis_index("dev").astype(jnp.int32)[None],
-            owner[:1],
-            iface_sizes,
-            shared_counts[0],
-            (neighbours[0] >= 0).astype(jnp.int32),
-        ]
-    )
-    goal = jnp.zeros((8, LANES), F32).at[:loads, EXTRA : EXTRA + modes].set(coarse_rhs[0].T)
     vec = struct(8, nmax)
     face = [struct(8, cap)] * nm
     tiles = struct(n, 8, LANES)
     table = struct(blocks, LANES, dtype=jnp.int32)
-
-    def call(kernel, name, in_specs, outs, scratch, *args):
+    chunk = 256
+
+    def call(body, name, outs, scratch, sc, *args, dense=None):
+        stage = [pltpu.SMEM(sc.shape, sc.dtype)] + [pltpu.VMEM(a.shape, a.dtype) for a in args]
+        extra = [] if dense is None else [dense]
+        streams = [
+            pltpu.VMEM((nmax // chunk, chunk, nmax), jnp.bfloat16),
+            pltpu.SemaphoreType.DMA((nmax // chunk,)),
+            pltpu.VMEM((16, nmax), F32),
+            pltpu.VMEM((nmax // chunk, 16, chunk), jnp.bfloat16),
+        ]
+
+        def kernel(*refs):
+            refs = list(refs)
+            pop = lambda k: [refs.pop(0) for _ in range(k)]
+            ins, big, results = pop(len(stage)), pop(len(extra)), pop(len(outs))
+            local = pop(len(stage))
+            (sems,) = pop(1)
+            product = Product(big[0], *pop(4)) if big else None
+            copies = [pltpu.make_async_copy(a, b, sems.at[i]) for i, (a, b) in enumerate(zip(ins, local))]
+            for c in copies:
+                c.start()
+            if product:
+                product.start()
+            for c in copies:
+                c.wait()
+            body(product, *local, *results, *refs)
+
         return pl.pallas_call(
             kernel,
             out_shape=outs,
-            in_specs=in_specs,
+            in_specs=[ANY] * (len(stage) + len(extra)),
             out_specs=[VMEM] * len(outs),
-            scratch_shapes=scratch,
+            scratch_shapes=stage + [pltpu.SemaphoreType.DMA((len(stage),))] + (streams if extra else []) + scratch,
             compiler_params=params,
             name=name,
-        )(*args)
+        )(sc, *args, *extra)
 
     def exchange(parts):
         return [lax.ppermute(x, "dev", perm) for x, (_, _, perm) in zip(parts, pairs)]
@@ -512,64 +545,60 @@
     def everyone(x):
         return lax.all_to_all(x, "dev", 0, 0)
 
-    modes_c, rhs_c, code, inv, *send = call(
+    outs = [struct(16, dtype=jnp.int32), vec, vec, table, table] + face
+    sc, modes_c, rhs_c, code, inv, *send = pl.pallas_call(
         functools.partial(prepare_kernel, n, cap, faces),
-        "prepare",
-        [SMEM] + [VMEM] * 4,
-        [vec, vec, table, table] + face,
-        [pltpu.VMEM((8, nmax), F32)],
-        sc,
+        out_shape=outs,
+        in_specs=[SMEM] * 4 + [VMEM] * 4,
+        out_specs=[SMEM] + [VMEM] * (len(outs) - 1),
+        compiler_params=params,
+        name="prepare",
+    )(
+        owner,
+        iface_sizes,
+        shared_counts,
+        neighbours,
         iface_map,
         iface_map.reshape(blocks, LANES),
-        rigid_modes,
+        rigid_modes.reshape(modes * blocks, LANES),
         dual_local,
     )
     far = exchange(send)
     c_mat, tile = call(
-        functools.partial(row_kernel, n, cap, faces),
+        lambda _, *refs: row_kernel(n, cap, faces, *refs),
         "coarse_row",
-        [SMEM] + [VMEM] * (2 + nm),
         [struct(EXTRA, nmax), tiles],
         [],
         sc,
         modes_c,
-        goal,
+        coarse_rhs[0],
         *far,
     )
     recv = everyone(tile)
-    chunk = 256
-    dense = [
-        pltpu.VMEM((nmax // chunk, chunk, nmax), jnp.bfloat16),
-        pltpu.SemaphoreType.DMA((nmax // chunk,)),
-        pltpu.VMEM((16, nmax), F32),
-        pltpu.VMEM((nmax // chunk, 16, chunk), jnp.bfloat16),
-    ]
     side = n * PAD // 2
     x, y, q_mat, tile, *send = call(
         functools.partial(start_kernel, n, cap, faces),
         "start",
-        [SMEM, ANY] + [VMEM] * 5,
         [vec, vec, struct(n * PAD, LANES), tiles] + face,
-        dense + [pltpu.VMEM((8, side), F32), pltpu.VMEM((side, side), F32), pltpu.VMEM((side, side), F32)],
+        [pltpu.VMEM((8, side), F32), pltpu.VMEM((side, side), F32), pltpu.VMEM((side, side), F32)],
         sc,
-        dual_blocks,
         recv,
         c_mat,
         rhs_c,
         code,
         inv,
+        dense=dual_blocks,
     )
     state = []
     for kind in (0, 1, 2, 3):
         recv, far = everyone(tile), exchange(send)
-        args = (sc, dual_blocks, recv, c_mat, q_mat, code, inv, y, *far, *state)
-        specs = [SMEM, ANY] + [VMEM] * (len(args) - 2)
+        args = (sc, recv, c_mat, q_mat, code, inv, y, *far, *state)
         body = functools.partial(step_kernel, n, cap, faces, kind)
         buf = [pltpu.VMEM((8, nmax), F32)]
         if kind == 3:
-            return tuple(call(body, "last", specs, [struct(1, 8, nmax)] * 2, buf, *args))
+            return tuple(call(body, "last", [struct(1, 8, nmax)] * 2, buf, *args))
         outs = [vec] + ([vec, vec, vec, struct(8, LANES)] if kind else []) + [vec, tiles] + face
-        got = list(call(body, f"step{kind}", specs, outs, dense + buf, *args))
+        got = list(call(body, f"step{kind}", outs, buf, *args, dense=dual_blocks))
         w = got.pop(0)
         if kind:
             x, p, s, scal = got[:4]

time: 174 us -> 148 us (0.85)
  Pallas kernels: 77.8 us -> 55.7 us
  local copies, waits for them, and re-layouts: 7.39 us -> 4.42 us
  other arithmetic: 2.63 us -> 0 us
    pallas_call x7, Pallas kernels: 77.8 us -> 55.7 us  [the longest x6 52.2 us: call(): pl.pallas_call(kernel, out_shape=outs, in_specs=[ANY] * (len(stage) + len...]
    another operation x2 -> x0, other arithmetic: 1.97 us -> none
    concatenate x1 -> x0, local copies, waits for them, and re-layouts: 1.92 us -> none  [per_device(): jnp.concatenate([lax.axis_index('dev').astype(jnp.int32)[None], owner[:1]...]
  transfers between devices with their start and end apart: 29 -> 29, of which waited for: 18 -> 19; matrix products, arithmetic and copies ran while one was open for 2% -> 1% of each run, Pallas kernels for 0% -> 0%
where the time goes in v2:
time: 148 us
  Pallas kernels  55.7 us (38%)
  starting transfers between devices  51.5 us (35%)
  waiting for transfers between devices  22.9 us (15%)
  blocking collectives  11.5 us (8%)
  local copies, waits for them, and re-layouts  4.42 us (3%)
  between operations  1.7 us (1%)
    pallas_call x6, Pallas kernels, call(): pl.pallas_call(kernel, out_shape=outs, in_specs=[ANY] * (len(stage) + len...  52.2 us
    ppermute x25, starting transfers between devices, exchange(): lax.ppermute(x, 'dev', perm)  39.3 us
    ppermute x25, waiting for transfers between devices, exchange(): lax.ppermute(x, 'dev', perm)  22.9 us
    all_to_all x4, starting transfers between devices, everyone(): return lax.all_to_all(x, 'dev', 0, 0)  12.2 us
    all_to_all x1, blocking collectives, everyone(): return lax.all_to_all(x, 'dev', 0, 0)  11.5 us
    unnamed x59, local copies, waits for them, and re-layouts  4.42 us
    pallas_call x1, Pallas kernels, per_device(): pl.pallas_call(functools.partial(prepare_kernel, n, cap, faces), out_shap...  3.47 us
  transfers between devices with their start and end apart: 29, of which 19 were waited for; matrix products, arithmetic and copies ran while one was open for 1% of the time, Pallas kernels for 0%

profile of v2, /device:TPU:0, one launch (start us, length us, event | category | flops | bytes accessed | tf_op | source)
XLA Modules:
  0.0 147.6 jit_solution(15527924608554484934)
XLA Ops:
  1.3 3.5 %prepare.1 = (s32[16]{0:T(128)}, f32[8,3072]{1,0:T(8,128)}, f32[8,3072]{1,0:T(8,128)}, s32[24,128]{1,0:T(8,128)}, s32[24,128]{1,0:T(8,128)}, /*index=5*/f32[8,51...) custom-call(s32[32]{0:T(128)} %owner.1, s32[1]{0:T(128)S(6)} %copy.14.sizes, ...), custom_call_target="tpu_custom_call" | custom-call | tf_op jit(solution)/shard_map/prepare/pallas_call | solution.py:549
  5.3 6.6 %collective-permute-start.1 = (f32[8,512]{1,0:T(8,128)}, f32[8,512]{1,0:T(8,128)S(1)}, u32[]{:S(2)}, u32[]{:S(2)}) collective-permute-start(f32[8,512]{1,0:T(8,128)} %get-tuple-element.58), channel_id=1, source_target_pairs={{0,31},{1,2},{3,4},{5,6},{7,8},{9,10},{11,12},{13,14},{15,16},{17,... | collective-permute-start | bytes 49160 | tf_op jit(solution)/shard_map/ppermute | solution.py:543
  11.9 1.9 %collective-permute-start.3 = (f32[8,512]{1,0:T(8,128)}, f32[8,512]{1,0:T(8,128)S(1)}, u32[]{:S(2)}, u32[]{:S(2)}) collective-permute-start(f32[8,512]{1,0:T(8,128)} %get-tuple-element.60), channel_id=1, source_target_pairs={{0,28},{1,29},{2,30},{3,31},{4,8},{5,9},{6,10},{7,11},{12,16},{13,... | collective-permute-start | bytes 49160 | tf_op jit(solution)/shard_map/ppermute | solution.py:543
  13.8 1.3 copy.13
  15.9 2.7 %collective-permute-done.3.refs_6_ = f32[8,512]{1,0:T(8,128)S(1)} collective-permute-done((f32[8,512]{1,0:T(8,128)}, f32[8,512]{1,0:T(8,128)S(1)}, u32[]{:S(2)}, u32[]{:S(2)}) %collective-permute-start.3) | collective-permute-done | bytes 16416 | tf_op jit(solution)/shard_map/ppermute | solution.py:543
  19.3 2.4 %coarse_row.1 = (f32[64,3072]{1,0:T(8,128)}, f32[32,8,128]{2,1,0:T(8,128)}) custom-call(s32[16]{0:T(128)} %get-tuple-element.55.refs_0_, f32[8,3072]{1,0:T(8,128)} %get-tuple-element.56.refs_1_, f32[6,8]{1,0:T(8,128)} %bitcast.7, f32[8,512]{1,0:T(8,128)} %copy-done.14, f32[8,512]{1,0:T(8,128)} %copy-done.15, f32[8,512]{1,0:T(8,128)} %copy-done.16, ...), custom_call_target="tpu_custom_call" | custom-call | tf_op jit(solution)/shard_map/coarse_row/pallas_call | solution.py:532
  21.7 11.5 %all_to_all.25.refs_1_ = f32[32,8,128]{2,1,0:T(8,128)} all-to-all(f32[32,8,128]{2,1,0:T(8,128)} %get-tuple-element.62), channel_id=1, replica_groups=mesh['dev'=32] {'dev'}, dimensions={0} | all-to-all | bytes 262144 | tf_op jit(solution)/shard_map/all_to_all | solution.py:546
  33.2 16.3 %start.1 = (f32[8,3072]{1,0:T(8,128)}, f32[8,3072]{1,0:T(8,128)}, f32[256,128]{1,0:T(8,128)}, f32[32,8,128]{2,1,0:T(8,128)}, f32[8,512]{1,0:T(8,128)}, /*index=5...) custom-call(s32[16]{0:T(128)} %get-tuple-element.55.refs_0_, ...), custom_call_target="tpu_custom_call" | custom-call | tf_op jit(solution)/shard_map/start/pallas_call | solution.py:532
  49.5 2.8 %all-to-all-start.1 = ((f32[32,8,128]{2,1,0:T(8,128)}), f32[32,8,128]{2,1,0:T(8,128)S(1)}, u32[]{:S(2)}, u32[]{:S(2)}) async-start(f32[32,8,128]{2,1,0:T(8,128)} %get-tuple-element.67), calls=%async_computation.1 | async-start | bytes 262144 | tf_op jit(solution)/shard_map/all_to_all | solution.py:546
  52.3 5.4 %collective-permute-start.6 = (f32[8,512]{1,0:T(8,128)}, f32[8,512]{1,0:T(8,128)S(1)}, u32[]{:S(2)}, u32[]{:S(2)}) collective-permute-start(f32[8,512]{1,0:T(8,128)} %get-tuple-element.71), channel_id=1, source_target_pairs={{0,31},{1,2},{3,4},{5,6},{7,8},{9,10},{11,12},{13,14},{15,16},{17,... | collective-permute-start | bytes 49160 | tf_op jit(solution)/shard_map/ppermute | solution.py:543
  57.7 2.0 %collective-permute-start.8 = (f32[8,512]{1,0:T(8,128)}, f32[8,512]{1,0:T(8,128)S(1)}, u32[]{:S(2)}, u32[]{:S(2)}) collective-permute-start(f32[8,512]{1,0:T(8,128)} %get-tuple-element.73), channel_id=1, source_target_pairs={{0,28},{1,29},{2,30},{3,31},{4,8},{5,9},{6,10},{7,11},{12,16},{13,... | collective-permute-start | bytes 49160 | tf_op jit(solution)/shard_map/ppermute | solution.py:543
  60.5 1.2 collective-permute-done.7.refs_9_
  61.7 2.7 %collective-permute-done.8.refs_10_ = f32[8,512]{1,0:T(8,128)S(1)} collective-permute-done((f32[8,512]{1,0:T(8,128)}, f32[8,512]{1,0:T(8,128)S(1)}, u32[]{:S(2)}, u32[]{:S(2)}) %collective-permute-start.8) | collective-permute-done | bytes 16416 | tf_op jit(solution)/shard_map/ppermute | solution.py:543
  65.2 9.5 %step0.1 = (f32[8,3072]{1,0:T(8,128)}, f32[8,3072]{1,0:T(8,128)}, f32[32,8,128]{2,1,0:T(8,128)}, f32[8,512]{1,0:T(8,128)}, f32[8,512]{1,0:T(8,128)}, /*index=5*/...) custom-call(s32[16]{0:T(128)} %get-tuple-element.55.refs_0_, f32[32,8,128]{2,1,0:T(8,128)} %copy-done.2, ...), custom_call_target="tpu_custom_call" | custom-call | tf_op jit(solution)/shard_map/step0/pallas_call | solution.py:532
  74.7 3.1 %all-to-all-start.2 = ((f32[32,8,128]{2,1,0:T(8,128)}), f32[32,8,128]{2,1,0:T(8,128)S(1)}, u32[]{:S(2)}, u32[]{:S(2)}) async-start(f32[32,8,128]{2,1,0:T(8,128)} %get-tuple-element.75), calls=%async_computation.2 | async-start | bytes 262144 | tf_op jit(solution)/shard_map/all_to_all | solution.py:546
  78.1 5.3 %collective-permute-start.11 = (f32[8,512]{1,0:T(8,128)}, f32[8,512]{1,0:T(8,128)S(1)}, u32[]{:S(2)}, u32[]{:S(2)}) collective-permute-start(f32[8,512]{1,0:T(8,128)} %get-tuple-element.78), channel_id=1, source_target_pairs={{0,31},{1,2},{3,4},{5,6},{7,8},{9,10},{11,12},{13,14},{15,16},{17,... | collective-permute-start | bytes 49160 | tf_op jit(solution)/shard_map/ppermute | solution.py:543
  83.5 2.0 %collective-permute-start.13 = (f32[8,512]{1,0:T(8,128)}, f32[8,512]{1,0:T(8,128)S(1)}, u32[]{:S(2)}, u32[]{:S(2)}) collective-permute-start(f32[8,512]{1,0:T(8,128)} %get-tuple-element.80), channel_id=1, source_target_pairs={{0,28},{1,29},{2,30},{3,31},{4,8},{5,9},{6,10},{7,11},{12,16},{13,... | collective-permute-start | bytes 49160 | tf_op jit(solution)/shard_map/ppermute | solution.py:543
  86.2 1.2 collective-permute-done.12.refs_9_
  87.4 2.7 %collective-permute-done.13.refs_10_ = f32[8,512]{1,0:T(8,128)S(1)} collective-permute-done((f32[8,512]{1,0:T(8,128)}, f32[8,512]{1,0:T(8,128)S(1)}, u32[]{:S(2)}, u32[]{:S(2)}) %collective-permute-start.13) | collective-permute-done | bytes 16416 | tf_op jit(solution)/shard_map/ppermute | solution.py:543
  90.9 9.6 %step1.1 = (f32[8,3072]{1,0:T(8,128)}, f32[8,3072]{1,0:T(8,128)}, f32[8,3072]{1,0:T(8,128)}, f32[8,3072]{1,0:T(8,128)}, f32[8,128]{1,0:T(8,128)}, /*index=5*/f32...) custom-call(s32[16]{0:T(128)} %get-tuple-element.55.refs_0_, ...), custom_call_target="tpu_custom_call" | custom-call | tf_op jit(solution)/shard_map/step1/pallas_call | solution.py:532
  100.5 3.1 %all-to-all-start.3 = ((f32[32,8,128]{2,1,0:T(8,128)}), f32[32,8,128]{2,1,0:T(8,128)S(1)}, u32[]{:S(2)}, u32[]{:S(2)}) async-start(f32[32,8,128]{2,1,0:T(8,128)} %get-tuple-element.84), calls=%async_computation.3 | async-start | bytes 262144 | tf_op jit(solution)/shard_map/all_to_all | solution.py:546
  103.9 5.3 %collective-permute-start.16 = (f32[8,512]{1,0:T(8,128)}, f32[8,512]{1,0:T(8,128)S(1)}, u32[]{:S(2)}, u32[]{:S(2)}) collective-permute-start(f32[8,512]{1,0:T(8,128)} %get-tuple-element.87), channel_id=1, source_target_pairs={{0,31},{1,2},{3,4},{5,6},{7,8},{9,10},{11,12},{13,14},{15,16},{17,... | collective-permute-start | bytes 49160 | tf_op jit(solution)/shard_map/ppermute | solution.py:543
  109.3 2.0 %collective-permute-start.18 = (f32[8,512]{1,0:T(8,128)}, f32[8,512]{1,0:T(8,128)S(1)}, u32[]{:S(2)}, u32[]{:S(2)}) collective-permute-start(f32[8,512]{1,0:T(8,128)} %get-tuple-element.89), channel_id=1, source_target_pairs={{0,28},{1,29},{2,30},{3,31},{4,8},{5,9},{6,10},{7,11},{12,16},{13,... | collective-permute-start | bytes 49160 | tf_op jit(solution)/shard_map/ppermute | solution.py:543
  112.1 1.2 collective-permute-done.17.refs_9_
  113.2 2.7 %collective-permute-done.18.refs_10_ = f32[8,512]{1,0:T(8,128)S(1)} collective-permute-done((f32[8,512]{1,0:T(8,128)}, f32[8,512]{1,0:T(8,128)S(1)}, u32[]{:S(2)}, u32[]{:S(2)}) %collective-permute-start.18) | collective-permute-done | bytes 16416 | tf_op jit(solution)/shard_map/ppermute | solution.py:543
  116.7 9.6 %step2.1 = (f32[8,3072]{1,0:T(8,128)}, f32[8,3072]{1,0:T(8,128)}, f32[8,3072]{1,0:T(8,128)}, f32[8,3072]{1,0:T(8,128)}, f32[8,128]{1,0:T(8,128)}, /*index=5*/f32...) custom-call(s32[16]{0:T(128)} %get-tuple-element.55.refs_0_, ...), custom_call_target="tpu_custom_call" | custom-call | tf_op jit(solution)/shard_map/step2/pallas_call | solution.py:532
  126.4 3.1 %all-to-all-start.4 = ((f32[32,8,128]{2,1,0:T(8,128)}), f32[32,8,128]{2,1,0:T(8,128)S(1)}, u32[]{:S(2)}, u32[]{:S(2)}) async-start(f32[32,8,128]{2,1,0:T(8,128)} %get-tuple-element.96), calls=%async_computation.4 | async-start | bytes 262144 | tf_op jit(solution)/shard_map/all_to_all | solution.py:546
  129.9 5.3 %collective-permute-start.21 = (f32[8,512]{1,0:T(8,128)}, f32[8,512]{1,0:T(8,128)S(1)}, u32[]{:S(2)}, u32[]{:S(2)}) collective-permute-start(f32[8,512]{1,0:T(8,128)} %get-tuple-element.99), channel_id=1, source_target_pairs={{0,31},{1,2},{3,4},{5,6},{7,8},{9,10},{11,12},{13,14},{15,16},{17,... | collective-permute-start | bytes 49160 | tf_op jit(solution)/shard_map/ppermute | solution.py:543
  135.2 2.0 %collective-permute-start.23 = (f32[8,512]{1,0:T(8,128)}, f32[8,512]{1,0:T(8,128)S(1)}, u32[]{:S(2)}, u32[]{:S(2)}) collective-permute-start(f32[8,512]{1,0:T(8,128)} %get-tuple-element.101), channel_id=1, source_target_pairs={{0,28},{1,29},{2,30},{3,31},{4,8},{5,9},{6,10},{7,11},{12,16},{13,... | collective-permute-start | bytes 49160 | tf_op jit(solution)/shard_map/ppermute | solution.py:543
  138.0 1.2 collective-permute-done.22.refs_9_
  139.1 2.7 %collective-permute-done.23.refs_10_ = f32[8,512]{1,0:T(8,128)S(1)} collective-permute-done((f32[8,512]{1,0:T(8,128)}, f32[8,512]{1,0:T(8,128)S(1)}, u32[]{:S(2)}, u32[]{:S(2)}) %collective-permute-start.23) | collective-permute-done | bytes 16416 | tf_op jit(solution)/shard_map/ppermute | solution.py:543
  142.7 4.8 %last.1 = (f32[1,8,3072]{2,1,0:T(8,128)}, f32[1,8,3072]{2,1,0:T(8,128)}) custom-call(s32[16]{0:T(128)} %get-tuple-element.55.refs_0_, f32[32,8,128]{2,1,0:T(8,128)} %copy-done.3, f32[64,3072]{1,0:T(8,128)} %get-tuple-element.63.refs_2_, f32[256,128]{1,0:T(8,128)} %get-tuple-element.68.refs_3_, s32[24,128]{1,0:T(8,128)} %get-tuple-element.65.refs_4_, ...), custom_call_target="tpu_custom_call" | custom-call | tf_op jit(solution)/shard_map/last/pallas_call | solution.py:532
  (93 shorter events, 9.4 us)
Async XLA Ops:
  4.8 10.3 %collective-permute-start = (f32[8,512]{1,0:T(8,128)}, f32[8,512]{1,0:T(8,128)S(1)}, u32[]{:S(2)}, u32[]{:S(2)}) collective-permute-start(f32[8,512]{1,0:T(8,128)} %get-tuple-element.57), channel_id=1, source_target_pairs={{0,1},{2,3},{4,5},{6,7},{8,9},{10,11},{12,13},{14,15},{16,17},{18,... | collective-permute-start | bytes 49160 | tf_op jit(solution)/shard_map/ppermute | solution.py:543
  5.3 9.8 %collective-permute-start.1 = (f32[8,512]{1,0:T(8,128)}, f32[8,512]{1,0:T(8,128)S(1)}, u32[]{:S(2)}, u32[]{:S(2)}) collective-permute-start(f32[8,512]{1,0:T(8,128)} %get-tuple-element.58), channel_id=1, source_target_pairs={{0,31},{1,2},{3,4},{5,6},{7,8},{9,10},{11,12},{13,14},{15,16},{17,... | collective-permute-start | bytes 49160 | tf_op jit(solution)/shard_map/ppermute | solution.py:543
  11.9 3.9 %collective-permute-start.2 = (f32[8,512]{1,0:T(8,128)}, f32[8,512]{1,0:T(8,128)S(1)}, u32[]{:S(2)}, u32[]{:S(2)}) collective-permute-start(f32[8,512]{1,0:T(8,128)} %get-tuple-element.59), channel_id=1, source_target_pairs={{0,4},{1,5},{2,6},{3,7},{8,12},{9,13},{10,14},{11,15},{16,20},{17,... | collective-permute-start | bytes 49160 | tf_op jit(solution)/shard_map/ppermute | solution.py:543
  11.9 6.6 %collective-permute-start.3 = (f32[8,512]{1,0:T(8,128)}, f32[8,512]{1,0:T(8,128)S(1)}, u32[]{:S(2)}, u32[]{:S(2)}) collective-permute-start(f32[8,512]{1,0:T(8,128)} %get-tuple-element.60), channel_id=1, source_target_pairs={{0,28},{1,29},{2,30},{3,31},{4,8},{5,9},{6,10},{7,11},{12,16},{13,... | collective-permute-start | bytes 49160 | tf_op jit(solution)/shard_map/ppermute | solution.py:543
  13.8 4.8 %collective-permute-start.4 = (f32[8,512]{1,0:T(8,128)}, f32[8,512]{1,0:T(8,128)S(1)}, u32[]{:S(2)}, u32[]{:S(2)}) collective-permute-start(f32[8,512]{1,0:T(8,128)} %get-tuple-element.61), channel_id=1, source_target_pairs={{0,16},{1,17},{2,18},{3,19},{4,20},{5,21},{6,22},{7,23},{8,24},{9,... | collective-permute-start | bytes 49160 | tf_op jit(solution)/shard_map/ppermute | solution.py:543
  49.5 15.1 %all-to-all-start.1 = ((f32[32,8,128]{2,1,0:T(8,128)}), f32[32,8,128]{2,1,0:T(8,128)S(1)}, u32[]{:S(2)}, u32[]{:S(2)}) async-start(f32[32,8,128]{2,1,0:T(8,128)} %get-tuple-element.67), calls=%async_computation.1 | async-start | bytes 262144 | tf_op jit(solution)/shard_map/all_to_all | solution.py:546
  52.2 7.4 %collective-permute-start.5 = (f32[8,512]{1,0:T(8,128)}, f32[8,512]{1,0:T(8,128)S(1)}, u32[]{:S(2)}, u32[]{:S(2)}) collective-permute-start(f32[8,512]{1,0:T(8,128)} %get-tuple-element.70), channel_id=1, source_target_pairs={{0,1},{2,3},{4,5},{6,7},{8,9},{10,11},{12,13},{14,15},{16,17},{18,... | collective-permute-start | bytes 49160 | tf_op jit(solution)/shard_map/ppermute | solution.py:543
  52.3 8.2 %collective-permute-start.6 = (f32[8,512]{1,0:T(8,128)}, f32[8,512]{1,0:T(8,128)S(1)}, u32[]{:S(2)}, u32[]{:S(2)}) collective-permute-start(f32[8,512]{1,0:T(8,128)} %get-tuple-element.71), channel_id=1, source_target_pairs={{0,31},{1,2},{3,4},{5,6},{7,8},{9,10},{11,12},{13,14},{15,16},{17,... | collective-permute-start | bytes 49160 | tf_op jit(solution)/shard_map/ppermute | solution.py:543
  57.7 3.9 %collective-permute-start.7 = (f32[8,512]{1,0:T(8,128)}, f32[8,512]{1,0:T(8,128)S(1)}, u32[]{:S(2)}, u32[]{:S(2)}) collective-permute-start(f32[8,512]{1,0:T(8,128)} %get-tuple-element.72), channel_id=1, source_target_pairs={{0,4},{1,5},{2,6},{3,7},{8,12},{9,13},{10,14},{11,15},{16,20},{17,... | collective-permute-start | bytes 49160 | tf_op jit(solution)/shard_map/ppermute | solution.py:543
  57.7 6.6 %collective-permute-start.8 = (f32[8,512]{1,0:T(8,128)}, f32[8,512]{1,0:T(8,128)S(1)}, u32[]{:S(2)}, u32[]{:S(2)}) collective-permute-start(f32[8,512]{1,0:T(8,128)} %get-tuple-element.73), channel_id=1, source_target_pairs={{0,28},{1,29},{2,30},{3,31},{4,8},{5,9},{6,10},{7,11},{12,16},{13,... | collective-permute-start | bytes 49160 | tf_op jit(solution)/shard_map/ppermute | solution.py:543
  59.7 4.8 %collective-permute-start.9 = (f32[8,512]{1,0:T(8,128)}, f32[8,512]{1,0:T(8,128)S(1)}, u32[]{:S(2)}, u32[]{:S(2)}) collective-permute-start(f32[8,512]{1,0:T(8,128)} %get-tuple-element.74), channel_id=1, source_target_pairs={{0,16},{1,17},{2,18},{3,19},{4,20},{5,21},{6,22},{7,23},{8,24},{9,... | collective-permute-start | bytes 49160 | tf_op jit(solution)/shard_map/ppermute | solution.py:543
  59.7 4.9 %copy-start.22 = (f32[8,512]{1,0:T(8,128)}, f32[8,512]{1,0:T(8,128)S(1)}, u32[]{:S(2)}) copy-start(f32[8,512]{1,0:T(8,128)S(1)} %collective-permute-done.5.refs_7_) | copy-start | bytes 49156
  74.7 15.6 %all-to-all-start.2 = ((f32[32,8,128]{2,1,0:T(8,128)}), f32[32,8,128]{2,1,0:T(8,128)S(1)}, u32[]{:S(2)}, u32[]{:S(2)}) async-start(f32[32,8,128]{2,1,0:T(8,128)} %get-tuple-element.75), calls=%async_computation.2 | async-start | bytes 262144 | tf_op jit(solution)/shard_map/all_to_all | solution.py:546
  77.8 7.6 %collective-permute-start.10 = (f32[8,512]{1,0:T(8,128)}, f32[8,512]{1,0:T(8,128)S(1)}, u32[]{:S(2)}, u32[]{:S(2)}) collective-permute-start(f32[8,512]{1,0:T(8,128)} %get-tuple-element.77), channel_id=1, source_target_pairs={{0,1},{2,3},{4,5},{6,7},{8,9},{10,11},{12,13},{14,15},{16,17},{18,... | collective-permute-start | bytes 49160 | tf_op jit(solution)/shard_map/ppermute | solution.py:543
  78.1 8.1 %collective-permute-start.11 = (f32[8,512]{1,0:T(8,128)}, f32[8,512]{1,0:T(8,128)S(1)}, u32[]{:S(2)}, u32[]{:S(2)}) collective-permute-start(f32[8,512]{1,0:T(8,128)} %get-tuple-element.78), channel_id=1, source_target_pairs={{0,31},{1,2},{3,4},{5,6},{7,8},{9,10},{11,12},{13,14},{15,16},{17,... | collective-permute-start | bytes 49160 | tf_op jit(solution)/shard_map/ppermute | solution.py:543
  83.5 3.9 %collective-permute-start.12 = (f32[8,512]{1,0:T(8,128)}, f32[8,512]{1,0:T(8,128)S(1)}, u32[]{:S(2)}, u32[]{:S(2)}) collective-permute-start(f32[8,512]{1,0:T(8,128)} %get-tuple-element.79), channel_id=1, source_target_pairs={{0,4},{1,5},{2,6},{3,7},{8,12},{9,13},{10,14},{11,15},{16,20},{17,... | collective-permute-start | bytes 49160 | tf_op jit(solution)/shard_map/ppermute | solution.py:543
  83.5 6.6 %collective-permute-start.13 = (f32[8,512]{1,0:T(8,128)}, f32[8,512]{1,0:T(8,128)S(1)}, u32[]{:S(2)}, u32[]{:S(2)}) collective-permute-start(f32[8,512]{1,0:T(8,128)} %get-tuple-element.80), channel_id=1, source_target_pairs={{0,28},{1,29},{2,30},{3,31},{4,8},{5,9},{6,10},{7,11},{12,16},{13,... | collective-permute-start | bytes 49160 | tf_op jit(solution)/shard_map/ppermute | solution.py:543
  85.4 4.8 %collective-permute-start.14 = (f32[8,512]{1,0:T(8,128)}, f32[8,512]{1,0:T(8,128)S(1)}, u32[]{:S(2)}, u32[]{:S(2)}) collective-permute-start(f32[8,512]{1,0:T(8,128)} %get-tuple-element.81), channel_id=1, source_target_pairs={{0,16},{1,17},{2,18},{3,19},{4,20},{5,21},{6,22},{7,23},{8,24},{9,... | collective-permute-start | bytes 49160 | tf_op jit(solution)/shard_map/ppermute | solution.py:543
  85.4 4.9 %copy-start.19 = (f32[8,512]{1,0:T(8,128)}, f32[8,512]{1,0:T(8,128)S(1)}, u32[]{:S(2)}) copy-start(f32[8,512]{1,0:T(8,128)S(1)} %collective-permute-done.10.refs_7_) | copy-start | bytes 49156
  100.5 15.6 %all-to-all-start.3 = ((f32[32,8,128]{2,1,0:T(8,128)}), f32[32,8,128]{2,1,0:T(8,128)S(1)}, u32[]{:S(2)}, u32[]{:S(2)}) async-start(f32[32,8,128]{2,1,0:T(8,128)} %get-tuple-element.84), calls=%async_computation.3 | async-start | bytes 262144 | tf_op jit(solution)/shard_map/all_to_all | solution.py:546
  103.6 7.6 %collective-permute-start.15 = (f32[8,512]{1,0:T(8,128)}, f32[8,512]{1,0:T(8,128)S(1)}, u32[]{:S(2)}, u32[]{:S(2)}) collective-permute-start(f32[8,512]{1,0:T(8,128)} %get-tuple-element.86), channel_id=1, source_target_pairs={{0,1},{2,3},{4,5},{6,7},{8,9},{10,11},{12,13},{14,15},{16,17},{18,... | collective-permute-start | bytes 49160 | tf_op jit(solution)/shard_map/ppermute | solution.py:543
  103.9 8.1 %collective-permute-start.16 = (f32[8,512]{1,0:T(8,128)}, f32[8,512]{1,0:T(8,128)S(1)}, u32[]{:S(2)}, u32[]{:S(2)}) collective-permute-start(f32[8,512]{1,0:T(8,128)} %get-tuple-element.87), channel_id=1, source_target_pairs={{0,31},{1,2},{3,4},{5,6},{7,8},{9,10},{11,12},{13,14},{15,16},{17,... | collective-permute-start | bytes 49160 | tf_op jit(solution)/shard_map/ppermute | solution.py:543
  109.3 3.9 %collective-permute-start.17 = (f32[8,512]{1,0:T(8,128)}, f32[8,512]{1,0:T(8,128)S(1)}, u32[]{:S(2)}, u32[]{:S(2)}) collective-permute-start(f32[8,512]{1,0:T(8,128)} %get-tuple-element.88), channel_id=1, source_target_pairs={{0,4},{1,5},{2,6},{3,7},{8,12},{9,13},{10,14},{11,15},{16,20},{17,... | collective-permute-start | bytes 49160 | tf_op jit(solution)/shard_map/ppermute | solution.py:543
  109.3 6.6 %collective-permute-start.18 = (f32[8,512]{1,0:T(8,128)}, f32[8,512]{1,0:T(8,128)S(1)}, u32[]{:S(2)}, u32[]{:S(2)}) collective-permute-start(f32[8,512]{1,0:T(8,128)} %get-tuple-element.89), channel_id=1, source_target_pairs={{0,28},{1,29},{2,30},{3,31},{4,8},{5,9},{6,10},{7,11},{12,16},{13,... | collective-permute-start | bytes 49160 | tf_op jit(solution)/shard_map/ppermute | solution.py:543
  111.2 4.8 %collective-permute-start.19 = (f32[8,512]{1,0:T(8,128)}, f32[8,512]{1,0:T(8,128)S(1)}, u32[]{:S(2)}, u32[]{:S(2)}) collective-permute-start(f32[8,512]{1,0:T(8,128)} %get-tuple-element.90), channel_id=1, source_target_pairs={{0,16},{1,17},{2,18},{3,19},{4,20},{5,21},{6,22},{7,23},{8,24},{9,... | collective-permute-start | bytes 49160 | tf_op jit(solution)/shard_map/ppermute | solution.py:543
  111.2 4.9 %copy-start.4 = (f32[8,512]{1,0:T(8,128)}, f32[8,512]{1,0:T(8,128)S(1)}, u32[]{:S(2)}) copy-start(f32[8,512]{1,0:T(8,128)S(1)} %collective-permute-done.15.refs_7_) | copy-start | bytes 49156
  126.4 15.6 %all-to-all-start.4 = ((f32[32,8,128]{2,1,0:T(8,128)}), f32[32,8,128]{2,1,0:T(8,128)S(1)}, u32[]{:S(2)}, u32[]{:S(2)}) async-start(f32[32,8,128]{2,1,0:T(8,128)} %get-tuple-element.96), calls=%async_computation.4 | async-start | bytes 262144 | tf_op jit(solution)/shard_map/all_to_all | solution.py:546
  129.5 7.6 %collective-permute-start.20 = (f32[8,512]{1,0:T(8,128)}, f32[8,512]{1,0:T(8,128)S(1)}, u32[]{:S(2)}, u32[]{:S(2)}) collective-permute-start(f32[8,512]{1,0:T(8,128)} %get-tuple-element.98), channel_id=1, source_target_pairs={{0,1},{2,3},{4,5},{6,7},{8,9},{10,11},{12,13},{14,15},{16,17},{18,... | collective-permute-start | bytes 49160 | tf_op jit(solution)/shard_map/ppermute | solution.py:543
  129.9 8.1 %collective-permute-start.21 = (f32[8,512]{1,0:T(8,128)}, f32[8,512]{1,0:T(8,128)S(1)}, u32[]{:S(2)}, u32[]{:S(2)}) collective-permute-start(f32[8,512]{1,0:T(8,128)} %get-tuple-element.99), channel_id=1, source_target_pairs={{0,31},{1,2},{3,4},{5,6},{7,8},{9,10},{11,12},{13,14},{15,16},{17,... | collective-permute-start | bytes 49160 | tf_op jit(solution)/shard_map/ppermute | solution.py:543
  135.2 3.9 %collective-permute-start.22 = (f32[8,512]{1,0:T(8,128)}, f32[8,512]{1,0:T(8,128)S(1)}, u32[]{:S(2)}, u32[]{:S(2)}) collective-permute-start(f32[8,512]{1,0:T(8,128)} %get-tuple-element.100), channel_id=1, source_target_pairs={{0,4},{1,5},{2,6},{3,7},{8,12},{9,13},{10,14},{11,15},{16,20},{17,... | collective-permute-start | bytes 49160 | tf_op jit(solution)/shard_map/ppermute | solution.py:543
  135.2 6.6 %collective-permute-start.23 = (f32[8,512]{1,0:T(8,128)}, f32[8,512]{1,0:T(8,128)S(1)}, u32[]{:S(2)}, u32[]{:S(2)}) collective-permute-start(f32[8,512]{1,0:T(8,128)} %get-tuple-element.101), channel_id=1, source_target_pairs={{0,28},{1,29},{2,30},{3,31},{4,8},{5,9},{6,10},{7,11},{12,16},{13,... | collective-permute-start | bytes 49160 | tf_op jit(solution)/shard_map/ppermute | solution.py:543
  137.1 4.8 %collective-permute-start.24 = (f32[8,512]{1,0:T(8,128)}, f32[8,512]{1,0:T(8,128)S(1)}, u32[]{:S(2)}, u32[]{:S(2)}) collective-permute-start(f32[8,512]{1,0:T(8,128)} %get-tuple-element.102), channel_id=1, source_target_pairs={{0,16},{1,17},{2,18},{3,19},{4,20},{5,21},{6,22},{7,23},{8,24},{9,... | collective-permute-start | bytes 49160 | tf_op jit(solution)/shard_map/ppermute | solution.py:543
  (26 other events, 51.1 us)

commit v3 on v2

--- a/solution.py
+++ b/solution.py
@@ -42,10 +42,10 @@
     return jnp.take_along_axis(x, idx, axis=1, mode="promise_in_bounds")
 
 
-def permute(load, table, blocks):
+def permute(load, table, blocks, which=None):
     tiles = [load(b) for b in range(blocks)]
     out = []
-    for b in range(blocks):
+    for b in range(blocks) if which is None else which:
         row = jnp.broadcast_to(table[b : b + 1, :], (8, LANES))
         high, low = row >> 7, row & 127
         acc = jnp.zeros((8, LANES), F32)
@@ -94,7 +94,21 @@
     hit = jnp.zeros((LANES, width), jnp.bool_)
     for b, step in enumerate((0,) + STEPS):
         hit = hit | ((row >> 3 == b) & (col == (step % n) * PAD + (row & 7)))
-    return jnp.where(hit, 1.0, 0.0).astype(F32)
+    return jnp.where(hit, 1.0, 0.0).astype(jnp.bfloat16)
+
+
+def halves(x):
+    high = x.astype(jnp.bfloat16)
+    return high, (x - high.astype(F32)).astype(jnp.bfloat16)
+
+
+def stacked(x):
+    return jnp.concatenate(halves(x), axis=0)
+
+
+def modes_times(z, c_ref):
+    r = dot(stacked(z), c_ref[...], precision=None)
+    return r[:8] + r[8:]
 
 
 def prepare_kernel(n, cap, faces, owner, sizes, counts, links, map_row, map_tile, modes, rhs, sc, *refs):
@@ -144,7 +158,7 @@
 
 def row_kernel(n, cap, faces, sc, modes, goal, *refs):
     nm = len(pairings(n)[0])
-    ins, (c_out, tile_out) = refs[:nm], refs[nm:]
+    ins, (c_half, tile_out, c_out) = refs[:nm], refs[nm:]
     fc = Faces(sc, n, cap)
     c_out[...] = jnp.zeros_like(c_out)
     c_out[0:PAD, :] = modes[...]
@@ -153,6 +167,7 @@
             at = f * cap + t * LANES
             c_out[PAD * (1 + f) : PAD * (2 + f), at : at + LANES] = -fc.far(ins, f, t)
     row = dot(modes[...], c_out[...], ((1,), (1,)))
+    c_half[...] = stacked(c_out[...])
     count = goal.shape[0]
     onehot = jnp.where(iota((count, LANES), 1) == iota((count, LANES), 0) + EXTRA, 1.0, 0.0).astype(F32)
     tile = jnp.concatenate([row, jnp.zeros((8, LANES - EXTRA), F32)], axis=1) + dot(goal[...], onehot, ((0,), (0,)))
@@ -300,7 +315,7 @@
         slot = slot_of(rr >> 3, black)
         hit = jnp.zeros((side, LANES), jnp.bool_)
         for b, step in enumerate((0,) + STEPS):
-            hit = hit | ((cc >> 3 == b) & (slot == lax.rem(sc[SLOT] + step + n, n)))
+            hit = hit | (((cc & 63) >> 3 == b) & (slot == lax.rem(sc[SLOT] + step + n, n)))
         sel.append(jnp.where(hit & ((rr & 7) == (cc & 7)), 1.0, 0.0).astype(F32))
     upper = dot(dd, sel[0]) + dot(ts, dot(t, sel[0], ((0,), (0,)))) - dot(ts, sel[1])
     lower = dot(sinv, sel[1]) - dot(ts, sel[0], ((0,), (0,)))
@@ -313,33 +328,50 @@
     return out
 
 
+def across(left, right, size, unit):
+    half = max(size // (2 * unit), 0) * unit
+    parts = [(0, half), (half, size)] if half else [(0, size)]
+    out = None
+    for a, b in parts:
+        v = dot(left(a, b), right(a, b), ((1,), (1,)), None)
+        out = v if out is None else out + v
+    return out
+
+
 class Product:
-    def __init__(self, b_hbm, b_vmem, sems, acc, vec):
-        self.b, self.acc, self.vec = b_vmem, acc, vec
-        self.chunks, rows = b_vmem.shape[:2]
-        self.copy = lambda k: pltpu.make_async_copy(b_hbm.at[0, pl.ds(k * rows, rows), :], b_vmem.at[k], sems.at[k])
+    def __init__(self, b_hbm, head, b_vmem, sems, acc, vec):
+        self.b, self.head, self.acc, self.vec = b_vmem, head, acc, vec
+        self.held = head.shape[0] // b_vmem.shape[1]
+        self.chunks, self.rows = b_vmem.shape[0] + self.held, b_vmem.shape[1]
+
+        def copy(k):
+            rows = pl.ds(k * self.rows, self.rows)
+            return pltpu.make_async_copy(b_hbm.at[0, rows, :], b_vmem.at[k - self.held], sems.at[k - self.held])
+
+        self.copy = copy
 
     def start(self):
         def one(k, carry):
             self.copy(k).start()
             return carry
 
-        lax.fori_loop(0, self.chunks, one, 0)
+        lax.fori_loop(self.held, self.chunks, one, 0)
 
     def __call__(self, tiles, code, inv):
-        acc, vec = self.acc, self.vec
+        acc, vec, rows = self.acc, self.vec, self.rows
         blocks = len(tiles)
-        moved = permute(lambda b: tiles[b], code, blocks)
-        per = blocks // self.chunks
+        per = rows // LANES
         for k in range(self.chunks):
-            v = jnp.concatenate(moved[k * per : (k + 1) * per], axis=1)
-            high = v.astype(jnp.bfloat16)
-            low = (v - high.astype(F32)).astype(jnp.bfloat16)
-            vec[k] = jnp.concatenate([high, low], axis=0)
-        for k in range(self.chunks):
-            self.copy(k).wait()
-            part = dot(vec[k], self.b[k], precision=None)
-            acc[...] = part if k == 0 else acc[...] + part
+            at, end = k * rows, (k + 1) * rows
+            moved = permute(lambda b: tiles[b], code, blocks, range(k * per, (k + 1) * per))
+            vec[:, at:end] = stacked(jnp.concatenate(moved, axis=1))
+            if k < self.held:
+                right = self.head[at:end, :]
+            else:
+                self.copy(k).wait()
+                right = self.b[k - self.held]
+            part = dot(vec[:, at:end], right, precision=None)
+            acc[...] = acc[...] + part if k else part
         return permute(lambda b: acc[0:8, b * LANES : (b + 1) * LANES] + acc[8:16, b * LANES : (b + 1) * LANES], inv, blocks)
 
 
@@ -361,7 +393,10 @@
 def coarse_of(n, recv, qloc):
     width = n * PAD
     rows = jnp.concatenate([recv[i] for i in range(n)], axis=0)
-    dense = dot(rows, spread(n, width))
+    high, rest = halves(rows)
+    middle, low = halves(rows - high.astype(F32))
+    where = spread(n, width)
+    dense = dot(jnp.concatenate([high, middle, low], axis=1), jnp.concatenate([where] * 3, axis=0), precision=None)
     goal = None
     both = None
     for i in range(n):
@@ -369,15 +404,16 @@
         x = x if i == 0 else pltpu.roll(x, i * PAD, 1)
         goal = x if goal is None else goal + x
         both = recv[i] if both is None else both + recv[i]
-    return dot(goal, qloc[...])[:, :EXTRA], both
-
-
-def finish(n, fc, y, extra, c_ref, ybuf, tile_out):
+    return dot(goal, qloc[...]), both
+
+
+def finish(n, y, extra, c_ref, vec, tile_out):
     for b, v in enumerate(y):
-        ybuf[:, b * LANES : (b + 1) * LANES] = v
-    row = dot(ybuf[...], c_ref[...], ((1,), (1,)))
-    tile = jnp.concatenate([row, jnp.zeros((8, LANES - EXTRA), F32)], axis=1)
+        vec[:, b * LANES : (b + 1) * LANES] = stacked(v)
+    row = across(lambda a, b: vec[:, a:b], lambda a, b: c_ref[:, a:b], vec.shape[1], 2 * LANES)
+    row = row[:8] + row[8:]
     lane = iota((8, LANES), 1)
+    tile = jnp.where(lane < EXTRA, row + pltpu.roll(row, EXTRA, 1), 0.0)
     for k, v in enumerate(extra):
         tile = jnp.where(lane == EXTRA + k, v, tile)
     for i in range(n):
@@ -399,16 +435,18 @@
             x = place(recv[i], EXTRA, (i * PAD) % LANES)
             v = x if v is None else v + x
         goal.append(v)
-    z = dot(jnp.concatenate(goal, axis=1), q_out[...])[:, :EXTRA]
-    lam_out[...] = dot(z, c_ref[...])
+    z = dot(jnp.concatenate(goal, axis=1), q_out[...])
+    lam_out[...] = modes_times(z, c_ref)
     y = product([lanes_of(lam_out, b) for b in range(blocks)], code, inv)
     t = [lanes_of(rhs, b) - y[b] for b in range(blocks)]
     fc.send(t, sends)
-    finish(n, fc, t, [], c_ref, t_out, tile_out)
+    for b in range(blocks):
+        t_out[:, b * LANES : (b + 1) * LANES] = t[b]
+    finish(n, t, [], c_ref, product.vec, tile_out)
 
 
 def assembled(fc, faces, c_ref, z, y_ref, far, buf):
-    buf[...] = dot(z, c_ref[...])
+    buf[...] = modes_times(z, c_ref)
     out = []
     for f in range(faces):
         for t in range(fc.per):
@@ -473,7 +511,9 @@
     extra = [total([weighted[b] * w[b] for b in range(blocks)]), total([w[b] * y[b] for b in range(blocks)])]
     if kind:
         extra.append(total([weighted[b] * lanes_of(s_out, b) + lanes_of(p_out, b) * y[b] for b in range(blocks)]))
-    finish(n, fc, y, extra, c_ref, y_out, tile_out)
+    for b in range(blocks):
+        y_out[:, b * LANES : (b + 1) * LANES] = y[b]
+    finish(n, y, extra, c_ref, product.vec, tile_out)
 
 
 VMEM = pl.BlockSpec(memory_space=pltpu.VMEM)
@@ -498,28 +538,32 @@
     nm = len(pairs)
     params = pltpu.CompilerParams(vmem_limit_bytes=56 * 1024 * 1024)
     vec = struct(8, nmax)
-    face = [struct(8, cap)] * nm
+    face = [pltpu.VMEM((8, cap), F32)] * nm
     tiles = struct(n, 8, LANES)
     table = struct(blocks, LANES, dtype=jnp.int32)
     chunk = 256
-
-    def call(body, name, outs, scratch, sc, *args, dense=None):
-        stage = [pltpu.SMEM(sc.shape, sc.dtype)] + [pltpu.VMEM(a.shape, a.dtype) for a in args]
-        extra = [] if dense is None else [dense]
+    held = 2
+    head = pltpu.with_memory_space_constraint(dual_blocks[0, : held * chunk], pltpu.VMEM)
+
+    def call(body, name, outs, scratch, sc, *args, dense=None, near=()):
+        far_args = [a for i, a in enumerate(args) if i not in near]
+        near_args = [pltpu.with_memory_space_constraint(args[i], pltpu.VMEM) for i in near]
+        stage = [pltpu.SMEM(sc.shape, sc.dtype)] + [pltpu.VMEM(a.shape, a.dtype) for a in far_args]
+        extra = [] if dense is None else [dense, head]
         streams = [
-            pltpu.VMEM((nmax // chunk, chunk, nmax), jnp.bfloat16),
-            pltpu.SemaphoreType.DMA((nmax // chunk,)),
+            pltpu.VMEM((nmax // chunk - held, chunk, nmax), jnp.bfloat16),
+            pltpu.SemaphoreType.DMA((nmax // chunk - held,)),
             pltpu.VMEM((16, nmax), F32),
-            pltpu.VMEM((nmax // chunk, 16, chunk), jnp.bfloat16),
+            pltpu.VMEM((16, nmax), jnp.bfloat16),
         ]
 
         def kernel(*refs):
             refs = list(refs)
             pop = lambda k: [refs.pop(0) for _ in range(k)]
-            ins, big, results = pop(len(stage)), pop(len(extra)), pop(len(outs))
+            ins, big, close, results = pop(len(stage)), pop(len(extra)), pop(len(near)), pop(len(outs))
             local = pop(len(stage))
             (sems,) = pop(1)
-            product = Product(big[0], *pop(4)) if big else None
+            product = Product(*big, *pop(4)) if big else None
             copies = [pltpu.make_async_copy(a, b, sems.at[i]) for i, (a, b) in enumerate(zip(ins, local))]
             for c in copies:
                 c.start()
@@ -527,17 +571,19 @@
                 product.start()
             for c in copies:
                 c.wait()
+            for i, ref in zip(near, close):
+                local.insert(i + 1, ref)
             body(product, *local, *results, *refs)
 
         return pl.pallas_call(
             kernel,
             out_shape=outs,
-            in_specs=[ANY] * (len(stage) + len(extra)),
+            in_specs=[ANY] * len(stage) + [ANY, VMEM][: len(extra)] + [VMEM] * len(near),
             out_specs=[VMEM] * len(outs),
             scratch_shapes=stage + [pltpu.SemaphoreType.DMA((len(stage),))] + (streams if extra else []) + scratch,
             compiler_params=params,
             name=name,
-        )(sc, *args, *extra)
+        )(sc, *far_args, *extra, *near_args)
 
     def exchange(parts):
         return [lax.ppermute(x, "dev", perm) for x, (_, _, perm) in zip(parts, pairs)]
@@ -567,12 +613,13 @@
     c_mat, tile = call(
         lambda _, *refs: row_kernel(n, cap, faces, *refs),
         "coarse_row",
-        [struct(EXTRA, nmax), tiles],
-        [],
+        [struct(2 * EXTRA, nmax, dtype=jnp.bfloat16), tiles],
+        [pltpu.VMEM((EXTRA, nmax), F32)],
         sc,
         modes_c,
         coarse_rhs[0],
         *far,
+        near=tuple(range(2, 2 + nm)),
     )
     recv = everyone(tile)
     side = n * PAD // 2
@@ -588,6 +635,7 @@
         code,
         inv,
         dense=dual_blocks,
+        near=(0,),
     )
     state = []
     for kind in (0, 1, 2, 3):
@@ -595,10 +643,11 @@
         args = (sc, recv, c_mat, q_mat, code, inv, y, *far, *state)
         body = functools.partial(step_kernel, n, cap, faces, kind)
         buf = [pltpu.VMEM((8, nmax), F32)]
+        near = (0,) + tuple(range(6, 6 + nm))
         if kind == 3:
-            return tuple(call(body, "last", [struct(1, 8, nmax)] * 2, buf, *args))
+            return tuple(call(body, "last", [struct(1, 8, nmax)] * 2, buf, *args, near=near))
         outs = [vec] + ([vec, vec, vec, struct(8, LANES)] if kind else []) + [vec, tiles] + face
-        got = list(call(body, f"step{kind}", outs, buf, *args, dense=dual_blocks))
+        got = list(call(body, f"step{kind}", outs, buf, *args, dense=dual_blocks, near=near))
         w = got.pop(0)
         if kind:
             x, p, s, scal = got[:4]

time: 148 us -> 138 us (0.932)
  blocking collectives: 11.5 us -> 0 us
  Pallas kernels: 55.7 us -> 49.5 us
  waiting for transfers between devices: 22.9 us -> 28 us
  starting transfers between devices: 51.5 us -> 54.7 us
    all_to_all x1 -> x0, blocking collectives: 11.5 us -> none  [everyone(): return lax.all_to_all(x, 'dev', 0, 0)]
    pallas_call x6, Pallas kernels: 52.2 us -> 46 us  [call(): pl.pallas_call(kernel, out_shape=outs, in_specs=[ANY] * len(stage) + [ANY...]
    all_to_all x4 -> x5, waiting for transfers between devices: 0.01 us -> 6.12 us  [everyone(): return lax.all_to_all(x, 'dev', 0, 0)]
    all_to_all x4 -> x5, starting transfers between devices: 12.2 us -> 15.6 us  [everyone(): return lax.all_to_all(x, 'dev', 0, 0)]
    unnamed x59 -> x1, local copies, waits for them, and re-layouts: 4.42 us -> 1.28 us
    squeeze x0 -> x1, local copies, waits for them, and re-layouts: none -> 2.1 us  [per_device(): dual_blocks[0, :held * chunk]]
  transfers between devices with their start and end apart: 29 -> 30, of which waited for: 19 -> 20; matrix products, arithmetic and copies ran while one was open for 1% -> 2% of each run, Pallas kernels for 0% -> 0%
where the time goes in v3:
time: 138 us; the launch traced here: 137 us
  starting transfers between devices  54.7 us (40%)
  Pallas kernels  49.5 us (36%)
  waiting for transfers between devices  28 us (20%)
  local copies, waits for them, and re-layouts  3.38 us (2%)
  between operations  1.58 us (1%)
    pallas_call x6, Pallas kernels, call(): pl.pallas_call(kernel, out_shape=outs, in_specs=[ANY] * len(stage) + [ANY...  46 us
    ppermute x25, starting transfers between devices, exchange(): lax.ppermute(x, 'dev', perm)  39.1 us
    ppermute x25, waiting for transfers between devices, exchange(): lax.ppermute(x, 'dev', perm)  21.9 us
    all_to_all x5, starting transfers between devices, everyone(): return lax.all_to_all(x, 'dev', 0, 0)  15.6 us
    all_to_all x5, waiting for transfers between devices, everyone(): return lax.all_to_all(x, 'dev', 0, 0)  6.12 us
    pallas_call x1, Pallas kernels, per_device(): pl.pallas_call(functools.partial(prepare_kernel, n, cap, faces), out_shap...  3.47 us
  transfers between devices with their start and end apart: 30, of which 20 were waited for; matrix products, arithmetic and copies ran while one was open for 2% of the time, Pallas kernels for 0%

profile of v3, /device:TPU:0, one launch (start us, length us, event | category | flops | bytes accessed | tf_op | source)
XLA Modules:
  0.0 137.1 jit_solution(11427097191343458452)
XLA Ops:
  1.3 3.5 %prepare.1 = (s32[16]{0:T(128)}, f32[8,3072]{1,0:T(8,128)}, f32[8,3072]{1,0:T(8,128)}, s32[24,128]{1,0:T(8,128)}, s32[24,128]{1,0:T(8,128)}, /*index=5*/f32[8,51...) custom-call(s32[32]{0:T(128)} %owner.1, ...), custom_call_target="tpu_custom_call" | custom-call | tf_op jit(solution)/shard_map/prepare/pallas_call | solution.py:595
  5.3 6.6 %collective-permute-start.1 = (f32[8,512]{1,0:T(8,128)S(1)}, f32[8,512]{1,0:T(8,128)S(1)}, u32[]{:S(2)}, u32[]{:S(2)}) collective-permute-start(f32[8,512]{1,0:T(8,128)S(1)} %get-tuple-element.58), channel_id=1, source_target_pairs={{0,31},{1,2},{3,4},{5,6},{7,8},{9,10},{11,12},{13,14},{15,16},{17,... | collective-permute-start | bytes 49160 | tf_op jit(solution)/shard_map/ppermute | solution.py:589
  11.9 1.9 %collective-permute-start.3 = (f32[8,512]{1,0:T(8,128)S(1)}, f32[8,512]{1,0:T(8,128)S(1)}, u32[]{:S(2)}, u32[]{:S(2)}) collective-permute-start(f32[8,512]{1,0:T(8,128)S(1)} %get-tuple-element.60), channel_id=1, source_target_pairs={{0,28},{1,29},{2,30},{3,31},{4,8},{5,9},{6,10},{7,11},{12,16},{13,... | collective-permute-start | bytes 49160 | tf_op jit(solution)/shard_map/ppermute | solution.py:589
  13.8 1.3 copy.13
  15.6 2.7 %collective-permute-done.3.refs_6_ = f32[8,512]{1,0:T(8,128)S(1)} collective-permute-done((f32[8,512]{1,0:T(8,128)S(1)}, f32[8,512]{1,0:T(8,128)S(1)}, u32[]{:S(2)}, u32[]{:S(2)}) %collective-permute-start.3) | collective-permute-done | bytes 16416 | tf_op jit(solution)/shard_map/ppermute | solution.py:589
  18.4 2.3 %coarse_row.1 = (bf16[128,3072]{1,0:T(8,128)(2,1)}, f32[32,8,128]{2,1,0:T(8,128)}) custom-call(s32[16]{0:T(128)} %get-tuple-element.55.refs_0_, f32[8,3072]{1,0:T(8,128)} %get-tuple-element.56.refs_1_, f32[6,8]{1,0:T(8,128)} %bitcast.9, f32[8,512]{1,0:T(8,128)S(1)} %collective-permute-done.refs_3_, f32[8,512]{1,0:T(8,128)S(1)} %collective-permute-done.1.refs_4_, ...), custom_call_target="tpu_custom_call" | custom-call | tf_op jit(solution)/shard_map/coarse_row/pallas_call | solution.py:578
  20.7 3.2 %all-to-all-start = ((f32[32,8,128]{2,1,0:T(8,128)}), f32[32,8,128]{2,1,0:T(8,128)S(1)}, u32[]{:S(2)}, u32[]{:S(2)}) async-start(f32[32,8,128]{2,1,0:T(8,128)} %get-tuple-element.66), calls=%async_computation | async-start | bytes 262144 | tf_op jit(solution)/shard_map/all_to_all | solution.py:592
  23.9 2.1 %slice_bitcast_fusion.refs_6_.refs_7_.refs_9_.refs_12_ = bf16[512,3072]{1,0:T(8,128)(2,1)S(1)} fusion(bf16[1,3072,3072]{2,1,0:T(8,128)(2,1)} %refs_11_.1), kind=kLoop, calls=%fused_computation | loop fusion | bytes 6291456 | tf_op jit(solution)/shard_map/squeeze | solution.py:546
  26.0 6.1 %all-to-all-done.refs_7_ = f32[32,8,128]{2,1,0:T(8,128)S(1)} async-done(((f32[32,8,128]{2,1,0:T(8,128)}), f32[32,8,128]{2,1,0:T(8,128)S(1)}, u32[]{:S(2)}, u32[]{:S(2)}) %all-to-all-start) | async-done | bytes 131104 | tf_op jit(solution)/shard_map/all_to_all | solution.py:592
  32.1 14.2 %start.1 = (f32[8,3072]{1,0:T(8,128)}, f32[8,3072]{1,0:T(8,128)}, f32[256,128]{1,0:T(8,128)}, f32[32,8,128]{2,1,0:T(8,128)}, f32[8,512]{1,0:T(8,128)S(1)}, /*ind...) custom-call(s32[16]{0:T(128)} %get-tuple-element.55.refs_0_, ...), custom_call_target="tpu_custom_call" | custom-call | tf_op jit(solution)/shard_map/start/pallas_call | solution.py:578
  46.3 2.8 %all-to-all-start.1 = ((f32[32,8,128]{2,1,0:T(8,128)}), f32[32,8,128]{2,1,0:T(8,128)S(1)}, u32[]{:S(2)}, u32[]{:S(2)}) async-start(f32[32,8,128]{2,1,0:T(8,128)} %get-tuple-element.69), calls=%async_computation.1 | async-start | bytes 262144 | tf_op jit(solution)/shard_map/all_to_all | solution.py:592
  49.1 5.4 %collective-permute-start.6 = (f32[8,512]{1,0:T(8,128)S(1)}, f32[8,512]{1,0:T(8,128)S(1)}, u32[]{:S(2)}, u32[]{:S(2)}) collective-permute-start(f32[8,512]{1,0:T(8,128)S(1)} %get-tuple-element.71), channel_id=1, source_target_pairs={{0,31},{1,2},{3,4},{5,6},{7,8},{9,10},{11,12},{13,14},{15,16},{17,... | collective-permute-start | bytes 49160 | tf_op jit(solution)/shard_map/ppermute | solution.py:589
  54.5 2.0 %collective-permute-start.8 = (f32[8,512]{1,0:T(8,128)S(1)}, f32[8,512]{1,0:T(8,128)S(1)}, u32[]{:S(2)}, u32[]{:S(2)}) collective-permute-start(f32[8,512]{1,0:T(8,128)S(1)} %get-tuple-element.73), channel_id=1, source_target_pairs={{0,28},{1,29},{2,30},{3,31},{4,8},{5,9},{6,10},{7,11},{12,16},{13,... | collective-permute-start | bytes 49160 | tf_op jit(solution)/shard_map/ppermute | solution.py:589
  57.3 1.0 collective-permute-done.7.refs_11_
  58.3 2.7 %collective-permute-done.8.refs_12_ = f32[8,512]{1,0:T(8,128)S(1)} collective-permute-done((f32[8,512]{1,0:T(8,128)S(1)}, f32[8,512]{1,0:T(8,128)S(1)}, u32[]{:S(2)}, u32[]{:S(2)}) %collective-permute-start.8) | collective-permute-done | bytes 16416 | tf_op jit(solution)/shard_map/ppermute | solution.py:589
  61.1 8.5 %step0.1 = (f32[8,3072]{1,0:T(8,128)}, f32[8,3072]{1,0:T(8,128)}, f32[32,8,128]{2,1,0:T(8,128)}, f32[8,512]{1,0:T(8,128)S(1)}, f32[8,512]{1,0:T(8,128)S(1)}, /*i...) custom-call(s32[16]{0:T(128)} %get-tuple-element.55.refs_0_, ...), custom_call_target="tpu_custom_call" | custom-call | tf_op jit(solution)/shard_map/step0/pallas_call | solution.py:578
  69.6 3.1 %all-to-all-start.2 = ((f32[32,8,128]{2,1,0:T(8,128)}), f32[32,8,128]{2,1,0:T(8,128)S(1)}, u32[]{:S(2)}, u32[]{:S(2)}) async-start(f32[32,8,128]{2,1,0:T(8,128)} %get-tuple-element.78), calls=%async_computation.2 | async-start | bytes 262144 | tf_op jit(solution)/shard_map/all_to_all | solution.py:592
  73.1 5.3 %collective-permute-start.11 = (f32[8,512]{1,0:T(8,128)S(1)}, f32[8,512]{1,0:T(8,128)S(1)}, u32[]{:S(2)}, u32[]{:S(2)}) collective-permute-start(f32[8,512]{1,0:T(8,128)S(1)} %get-tuple-element.80), channel_id=1, source_target_pairs={{0,31},{1,2},{3,4},{5,6},{7,8},{9,10},{11,12},{13,14},{15,16},{17,... | collective-permute-start | bytes 49160 | tf_op jit(solution)/shard_map/ppermute | solution.py:589
  78.4 2.0 %collective-permute-start.13 = (f32[8,512]{1,0:T(8,128)S(1)}, f32[8,512]{1,0:T(8,128)S(1)}, u32[]{:S(2)}, u32[]{:S(2)}) collective-permute-start(f32[8,512]{1,0:T(8,128)S(1)} %get-tuple-element.82), channel_id=1, source_target_pairs={{0,28},{1,29},{2,30},{3,31},{4,8},{5,9},{6,10},{7,11},{12,16},{13,... | collective-permute-start | bytes 49160 | tf_op jit(solution)/shard_map/ppermute | solution.py:589
  82.1 2.7 %collective-permute-done.13.refs_14_ = f32[8,512]{1,0:T(8,128)S(1)} collective-permute-done((f32[8,512]{1,0:T(8,128)S(1)}, f32[8,512]{1,0:T(8,128)S(1)}, u32[]{:S(2)}, u32[]{:S(2)}) %collective-permute-start.13) | collective-permute-done | bytes 16416 | tf_op jit(solution)/shard_map/ppermute | solution.py:589
  85.0 8.6 %step1.1 = (f32[8,3072]{1,0:T(8,128)}, f32[8,3072]{1,0:T(8,128)}, f32[8,3072]{1,0:T(8,128)}, f32[8,3072]{1,0:T(8,128)}, f32[8,128]{1,0:T(8,128)}, /*index=5*/f32...) custom-call(s32[16]{0:T(128)} %get-tuple-element.55.refs_0_, ...), custom_call_target="tpu_custom_call" | custom-call | tf_op jit(solution)/shard_map/step1/pallas_call | solution.py:578
  93.6 3.4 %all-to-all-start.3 = ((f32[32,8,128]{2,1,0:T(8,128)}), f32[32,8,128]{2,1,0:T(8,128)S(1)}, u32[]{:S(2)}, u32[]{:S(2)}) async-start(f32[32,8,128]{2,1,0:T(8,128)} %get-tuple-element.90), calls=%async_computation.3 | async-start | bytes 262144 | tf_op jit(solution)/shard_map/all_to_all | solution.py:592
  97.0 5.3 %collective-permute-start.16 = (f32[8,512]{1,0:T(8,128)S(1)}, f32[8,512]{1,0:T(8,128)S(1)}, u32[]{:S(2)}, u32[]{:S(2)}) collective-permute-start(f32[8,512]{1,0:T(8,128)S(1)} %get-tuple-element.92), channel_id=1, source_target_pairs={{0,31},{1,2},{3,4},{5,6},{7,8},{9,10},{11,12},{13,14},{15,16},{17,... | collective-permute-start | bytes 49160 | tf_op jit(solution)/shard_map/ppermute | solution.py:589
  102.4 2.0 %collective-permute-start.18 = (f32[8,512]{1,0:T(8,128)S(1)}, f32[8,512]{1,0:T(8,128)S(1)}, u32[]{:S(2)}, u32[]{:S(2)}) collective-permute-start(f32[8,512]{1,0:T(8,128)S(1)} %get-tuple-element.94), channel_id=1, source_target_pairs={{0,28},{1,29},{2,30},{3,31},{4,8},{5,9},{6,10},{7,11},{12,16},{13,... | collective-permute-start | bytes 49160 | tf_op jit(solution)/shard_map/ppermute | solution.py:589
  105.1 1.0 collective-permute-done.17.refs_16_
  106.1 2.7 %collective-permute-done.18.refs_17_ = f32[8,512]{1,0:T(8,128)S(1)} collective-permute-done((f32[8,512]{1,0:T(8,128)S(1)}, f32[8,512]{1,0:T(8,128)S(1)}, u32[]{:S(2)}, u32[]{:S(2)}) %collective-permute-start.18) | collective-permute-done | bytes 16416 | tf_op jit(solution)/shard_map/ppermute | solution.py:589
  109.0 8.6 %step2.1 = (f32[8,3072]{1,0:T(8,128)}, f32[8,3072]{1,0:T(8,128)}, f32[8,3072]{1,0:T(8,128)}, f32[8,3072]{1,0:T(8,128)}, f32[8,128]{1,0:T(8,128)}, /*index=5*/f32...) custom-call(s32[16]{0:T(128)} %get-tuple-element.55.refs_0_, ...), custom_call_target="tpu_custom_call" | custom-call | tf_op jit(solution)/shard_map/step2/pallas_call | solution.py:578
  117.6 3.1 %all-to-all-start.4 = ((f32[32,8,128]{2,1,0:T(8,128)}), f32[32,8,128]{2,1,0:T(8,128)S(1)}, u32[]{:S(2)}, u32[]{:S(2)}) async-start(f32[32,8,128]{2,1,0:T(8,128)} %get-tuple-element.102), calls=%async_computation.4 | async-start | bytes 262144 | tf_op jit(solution)/shard_map/all_to_all | solution.py:592
  121.1 5.3 %collective-permute-start.21 = (f32[8,512]{1,0:T(8,128)S(1)}, f32[8,512]{1,0:T(8,128)S(1)}, u32[]{:S(2)}, u32[]{:S(2)}) collective-permute-start(f32[8,512]{1,0:T(8,128)S(1)} %get-tuple-element.104), channel_id=1, source_target_pairs={{0,31},{1,2},{3,4},{5,6},{7,8},{9,10},{11,12},{13,14},{15,16},{17,... | collective-permute-start | bytes 49160 | tf_op jit(solution)/shard_map/ppermute | solution.py:589
  126.4 2.0 %collective-permute-start.23 = (f32[8,512]{1,0:T(8,128)S(1)}, f32[8,512]{1,0:T(8,128)S(1)}, u32[]{:S(2)}, u32[]{:S(2)}) collective-permute-start(f32[8,512]{1,0:T(8,128)S(1)} %get-tuple-element.106), channel_id=1, source_target_pairs={{0,28},{1,29},{2,30},{3,31},{4,8},{5,9},{6,10},{7,11},{12,16},{13,... | collective-permute-start | bytes 49160 | tf_op jit(solution)/shard_map/ppermute | solution.py:589
  130.2 2.7 %collective-permute-done.23.refs_15_ = f32[8,512]{1,0:T(8,128)S(1)} collective-permute-done((f32[8,512]{1,0:T(8,128)S(1)}, f32[8,512]{1,0:T(8,128)S(1)}, u32[]{:S(2)}, u32[]{:S(2)}) %collective-permute-start.23) | collective-permute-done | bytes 16416 | tf_op jit(solution)/shard_map/ppermute | solution.py:589
  133.0 3.9 %last.1 = (f32[1,8,3072]{2,1,0:T(8,128)}, f32[1,8,3072]{2,1,0:T(8,128)}) custom-call(s32[16]{0:T(128)} %get-tuple-element.55.refs_0_, bf16[128,3072]{1,0:T(8,128)(2,1)} %get-tuple-element.62.refs_1_, f32[256,128]{1,0:T(8,128)} %get-tuple-element.67.refs_2_, s32[24,128]{1,0:T(8,128)} %get-tuple-element.64.refs_3_, s32[24,128]{1,0:T(8,128)} %get-tuple-element.65.refs_4_, ...), custom_call_target="tpu_custom_call" | custom-call | tf_op jit(solution)/shard_map/last/pallas_call | solution.py:578
  (37 shorter events, 7.8 us)
Async XLA Ops:
  4.8 10.3 %collective-permute-start = (f32[8,512]{1,0:T(8,128)S(1)}, f32[8,512]{1,0:T(8,128)S(1)}, u32[]{:S(2)}, u32[]{:S(2)}) collective-permute-start(f32[8,512]{1,0:T(8,128)S(1)} %get-tuple-element.57), channel_id=1, source_target_pairs={{0,1},{2,3},{4,5},{6,7},{8,9},{10,11},{12,13},{14,15},{16,17},{18,... | collective-permute-start | bytes 49160 | tf_op jit(solution)/shard_map/ppermute | solution.py:589
  5.3 9.8 %collective-permute-start.1 = (f32[8,512]{1,0:T(8,128)S(1)}, f32[8,512]{1,0:T(8,128)S(1)}, u32[]{:S(2)}, u32[]{:S(2)}) collective-permute-start(f32[8,512]{1,0:T(8,128)S(1)} %get-tuple-element.58), channel_id=1, source_target_pairs={{0,31},{1,2},{3,4},{5,6},{7,8},{9,10},{11,12},{13,14},{15,16},{17,... | collective-permute-start | bytes 49160 | tf_op jit(solution)/shard_map/ppermute | solution.py:589
  11.9 3.7 %collective-permute-start.2 = (f32[8,512]{1,0:T(8,128)S(1)}, f32[8,512]{1,0:T(8,128)S(1)}, u32[]{:S(2)}, u32[]{:S(2)}) collective-permute-start(f32[8,512]{1,0:T(8,128)S(1)} %get-tuple-element.59), channel_id=1, source_target_pairs={{0,4},{1,5},{2,6},{3,7},{8,12},{9,13},{10,14},{11,15},{16,20},{17,... | collective-permute-start | bytes 49160 | tf_op jit(solution)/shard_map/ppermute | solution.py:589
  11.9 6.4 %collective-permute-start.3 = (f32[8,512]{1,0:T(8,128)S(1)}, f32[8,512]{1,0:T(8,128)S(1)}, u32[]{:S(2)}, u32[]{:S(2)}) collective-permute-start(f32[8,512]{1,0:T(8,128)S(1)} %get-tuple-element.60), channel_id=1, source_target_pairs={{0,28},{1,29},{2,30},{3,31},{4,8},{5,9},{6,10},{7,11},{12,16},{13,... | collective-permute-start | bytes 49160 | tf_op jit(solution)/shard_map/ppermute | solution.py:589
  13.8 4.6 %collective-permute-start.4 = (f32[8,512]{1,0:T(8,128)S(1)}, f32[8,512]{1,0:T(8,128)S(1)}, u32[]{:S(2)}, u32[]{:S(2)}) collective-permute-start(f32[8,512]{1,0:T(8,128)S(1)} %get-tuple-element.61), channel_id=1, source_target_pairs={{0,16},{1,17},{2,18},{3,19},{4,20},{5,21},{6,22},{7,23},{8,24},{9,... | collective-permute-start | bytes 49160 | tf_op jit(solution)/shard_map/ppermute | solution.py:589
  20.7 11.4 %all-to-all-start = ((f32[32,8,128]{2,1,0:T(8,128)}), f32[32,8,128]{2,1,0:T(8,128)S(1)}, u32[]{:S(2)}, u32[]{:S(2)}) async-start(f32[32,8,128]{2,1,0:T(8,128)} %get-tuple-element.66), calls=%async_computation | async-start | bytes 262144 | tf_op jit(solution)/shard_map/all_to_all | solution.py:592
  46.3 14.9 %all-to-all-start.1 = ((f32[32,8,128]{2,1,0:T(8,128)}), f32[32,8,128]{2,1,0:T(8,128)S(1)}, u32[]{:S(2)}, u32[]{:S(2)}) async-start(f32[32,8,128]{2,1,0:T(8,128)} %get-tuple-element.69), calls=%async_computation.1 | async-start | bytes 262144 | tf_op jit(solution)/shard_map/all_to_all | solution.py:592
  49.1 7.4 %collective-permute-start.5 = (f32[8,512]{1,0:T(8,128)S(1)}, f32[8,512]{1,0:T(8,128)S(1)}, u32[]{:S(2)}, u32[]{:S(2)}) collective-permute-start(f32[8,512]{1,0:T(8,128)S(1)} %get-tuple-element.70), channel_id=1, source_target_pairs={{0,1},{2,3},{4,5},{6,7},{8,9},{10,11},{12,13},{14,15},{16,17},{18,... | collective-permute-start | bytes 49160 | tf_op jit(solution)/shard_map/ppermute | solution.py:589
  49.1 8.2 %collective-permute-start.6 = (f32[8,512]{1,0:T(8,128)S(1)}, f32[8,512]{1,0:T(8,128)S(1)}, u32[]{:S(2)}, u32[]{:S(2)}) collective-permute-start(f32[8,512]{1,0:T(8,128)S(1)} %get-tuple-element.71), channel_id=1, source_target_pairs={{0,31},{1,2},{3,4},{5,6},{7,8},{9,10},{11,12},{13,14},{15,16},{17,... | collective-permute-start | bytes 49160 | tf_op jit(solution)/shard_map/ppermute | solution.py:589
  54.5 3.7 %collective-permute-start.7 = (f32[8,512]{1,0:T(8,128)S(1)}, f32[8,512]{1,0:T(8,128)S(1)}, u32[]{:S(2)}, u32[]{:S(2)}) collective-permute-start(f32[8,512]{1,0:T(8,128)S(1)} %get-tuple-element.72), channel_id=1, source_target_pairs={{0,4},{1,5},{2,6},{3,7},{8,12},{9,13},{10,14},{11,15},{16,20},{17,... | collective-permute-start | bytes 49160 | tf_op jit(solution)/shard_map/ppermute | solution.py:589
  54.5 6.4 %collective-permute-start.8 = (f32[8,512]{1,0:T(8,128)S(1)}, f32[8,512]{1,0:T(8,128)S(1)}, u32[]{:S(2)}, u32[]{:S(2)}) collective-permute-start(f32[8,512]{1,0:T(8,128)S(1)} %get-tuple-element.73), channel_id=1, source_target_pairs={{0,28},{1,29},{2,30},{3,31},{4,8},{5,9},{6,10},{7,11},{12,16},{13,... | collective-permute-start | bytes 49160 | tf_op jit(solution)/shard_map/ppermute | solution.py:589
  56.5 4.6 %collective-permute-start.9 = (f32[8,512]{1,0:T(8,128)S(1)}, f32[8,512]{1,0:T(8,128)S(1)}, u32[]{:S(2)}, u32[]{:S(2)}) collective-permute-start(f32[8,512]{1,0:T(8,128)S(1)} %get-tuple-element.74), channel_id=1, source_target_pairs={{0,16},{1,17},{2,18},{3,19},{4,20},{5,21},{6,22},{7,23},{8,24},{9,... | collective-permute-start | bytes 49160 | tf_op jit(solution)/shard_map/ppermute | solution.py:589
  69.6 15.4 %all-to-all-start.2 = ((f32[32,8,128]{2,1,0:T(8,128)}), f32[32,8,128]{2,1,0:T(8,128)S(1)}, u32[]{:S(2)}, u32[]{:S(2)}) async-start(f32[32,8,128]{2,1,0:T(8,128)} %get-tuple-element.78), calls=%async_computation.2 | async-start | bytes 262144 | tf_op jit(solution)/shard_map/all_to_all | solution.py:592
  72.8 7.6 %collective-permute-start.10 = (f32[8,512]{1,0:T(8,128)S(1)}, f32[8,512]{1,0:T(8,128)S(1)}, u32[]{:S(2)}, u32[]{:S(2)}) collective-permute-start(f32[8,512]{1,0:T(8,128)S(1)} %get-tuple-element.79), channel_id=1, source_target_pairs={{0,1},{2,3},{4,5},{6,7},{8,9},{10,11},{12,13},{14,15},{16,17},{18,... | collective-permute-start | bytes 49160 | tf_op jit(solution)/shard_map/ppermute | solution.py:589
  73.1 8.1 %collective-permute-start.11 = (f32[8,512]{1,0:T(8,128)S(1)}, f32[8,512]{1,0:T(8,128)S(1)}, u32[]{:S(2)}, u32[]{:S(2)}) collective-permute-start(f32[8,512]{1,0:T(8,128)S(1)} %get-tuple-element.80), channel_id=1, source_target_pairs={{0,31},{1,2},{3,4},{5,6},{7,8},{9,10},{11,12},{13,14},{15,16},{17,... | collective-permute-start | bytes 49160 | tf_op jit(solution)/shard_map/ppermute | solution.py:589
  78.4 3.7 %collective-permute-start.12 = (f32[8,512]{1,0:T(8,128)S(1)}, f32[8,512]{1,0:T(8,128)S(1)}, u32[]{:S(2)}, u32[]{:S(2)}) collective-permute-start(f32[8,512]{1,0:T(8,128)S(1)} %get-tuple-element.81), channel_id=1, source_target_pairs={{0,4},{1,5},{2,6},{3,7},{8,12},{9,13},{10,14},{11,15},{16,20},{17,... | collective-permute-start | bytes 49160 | tf_op jit(solution)/shard_map/ppermute | solution.py:589
  78.4 6.4 %collective-permute-start.13 = (f32[8,512]{1,0:T(8,128)S(1)}, f32[8,512]{1,0:T(8,128)S(1)}, u32[]{:S(2)}, u32[]{:S(2)}) collective-permute-start(f32[8,512]{1,0:T(8,128)S(1)} %get-tuple-element.82), channel_id=1, source_target_pairs={{0,28},{1,29},{2,30},{3,31},{4,8},{5,9},{6,10},{7,11},{12,16},{13,... | collective-permute-start | bytes 49160 | tf_op jit(solution)/shard_map/ppermute | solution.py:589
  80.4 4.6 %collective-permute-start.14 = (f32[8,512]{1,0:T(8,128)S(1)}, f32[8,512]{1,0:T(8,128)S(1)}, u32[]{:S(2)}, u32[]{:S(2)}) collective-permute-start(f32[8,512]{1,0:T(8,128)S(1)} %get-tuple-element.83), channel_id=1, source_target_pairs={{0,16},{1,17},{2,18},{3,19},{4,20},{5,21},{6,22},{7,23},{8,24},{9,... | collective-permute-start | bytes 49160 | tf_op jit(solution)/shard_map/ppermute | solution.py:589
  93.6 15.4 %all-to-all-start.3 = ((f32[32,8,128]{2,1,0:T(8,128)}), f32[32,8,128]{2,1,0:T(8,128)S(1)}, u32[]{:S(2)}, u32[]{:S(2)}) async-start(f32[32,8,128]{2,1,0:T(8,128)} %get-tuple-element.90), calls=%async_computation.3 | async-start | bytes 262144 | tf_op jit(solution)/shard_map/all_to_all | solution.py:592
  96.9 7.4 %collective-permute-start.15 = (f32[8,512]{1,0:T(8,128)S(1)}, f32[8,512]{1,0:T(8,128)S(1)}, u32[]{:S(2)}, u32[]{:S(2)}) collective-permute-start(f32[8,512]{1,0:T(8,128)S(1)} %get-tuple-element.91), channel_id=1, source_target_pairs={{0,1},{2,3},{4,5},{6,7},{8,9},{10,11},{12,13},{14,15},{16,17},{18,... | collective-permute-start | bytes 49160 | tf_op jit(solution)/shard_map/ppermute | solution.py:589
  97.0 8.1 %collective-permute-start.16 = (f32[8,512]{1,0:T(8,128)S(1)}, f32[8,512]{1,0:T(8,128)S(1)}, u32[]{:S(2)}, u32[]{:S(2)}) collective-permute-start(f32[8,512]{1,0:T(8,128)S(1)} %get-tuple-element.92), channel_id=1, source_target_pairs={{0,31},{1,2},{3,4},{5,6},{7,8},{9,10},{11,12},{13,14},{15,16},{17,... | collective-permute-start | bytes 49160 | tf_op jit(solution)/shard_map/ppermute | solution.py:589
  102.4 3.7 %collective-permute-start.17 = (f32[8,512]{1,0:T(8,128)S(1)}, f32[8,512]{1,0:T(8,128)S(1)}, u32[]{:S(2)}, u32[]{:S(2)}) collective-permute-start(f32[8,512]{1,0:T(8,128)S(1)} %get-tuple-element.93), channel_id=1, source_target_pairs={{0,4},{1,5},{2,6},{3,7},{8,12},{9,13},{10,14},{11,15},{16,20},{17,... | collective-permute-start | bytes 49160 | tf_op jit(solution)/shard_map/ppermute | solution.py:589
  102.4 6.4 %collective-permute-start.18 = (f32[8,512]{1,0:T(8,128)S(1)}, f32[8,512]{1,0:T(8,128)S(1)}, u32[]{:S(2)}, u32[]{:S(2)}) collective-permute-start(f32[8,512]{1,0:T(8,128)S(1)} %get-tuple-element.94), channel_id=1, source_target_pairs={{0,28},{1,29},{2,30},{3,31},{4,8},{5,9},{6,10},{7,11},{12,16},{13,... | collective-permute-start | bytes 49160 | tf_op jit(solution)/shard_map/ppermute | solution.py:589
  104.3 4.6 %collective-permute-start.19 = (f32[8,512]{1,0:T(8,128)S(1)}, f32[8,512]{1,0:T(8,128)S(1)}, u32[]{:S(2)}, u32[]{:S(2)}) collective-permute-start(f32[8,512]{1,0:T(8,128)S(1)} %get-tuple-element.95), channel_id=1, source_target_pairs={{0,16},{1,17},{2,18},{3,19},{4,20},{5,21},{6,22},{7,23},{8,24},{9,... | collective-permute-start | bytes 49160 | tf_op jit(solution)/shard_map/ppermute | solution.py:589
  117.6 15.4 %all-to-all-start.4 = ((f32[32,8,128]{2,1,0:T(8,128)}), f32[32,8,128]{2,1,0:T(8,128)S(1)}, u32[]{:S(2)}, u32[]{:S(2)}) async-start(f32[32,8,128]{2,1,0:T(8,128)} %get-tuple-element.102), calls=%async_computation.4 | async-start | bytes 262144 | tf_op jit(solution)/shard_map/all_to_all | solution.py:592
  120.8 7.6 %collective-permute-start.20 = (f32[8,512]{1,0:T(8,128)S(1)}, f32[8,512]{1,0:T(8,128)S(1)}, u32[]{:S(2)}, u32[]{:S(2)}) collective-permute-start(f32[8,512]{1,0:T(8,128)S(1)} %get-tuple-element.103), channel_id=1, source_target_pairs={{0,1},{2,3},{4,5},{6,7},{8,9},{10,11},{12,13},{14,15},{16,17},{18,... | collective-permute-start | bytes 49160 | tf_op jit(solution)/shard_map/ppermute | solution.py:589
  121.1 8.1 %collective-permute-start.21 = (f32[8,512]{1,0:T(8,128)S(1)}, f32[8,512]{1,0:T(8,128)S(1)}, u32[]{:S(2)}, u32[]{:S(2)}) collective-permute-start(f32[8,512]{1,0:T(8,128)S(1)} %get-tuple-element.104), channel_id=1, source_target_pairs={{0,31},{1,2},{3,4},{5,6},{7,8},{9,10},{11,12},{13,14},{15,16},{17,... | collective-permute-start | bytes 49160 | tf_op jit(solution)/shard_map/ppermute | solution.py:589
  126.4 3.7 %collective-permute-start.22 = (f32[8,512]{1,0:T(8,128)S(1)}, f32[8,512]{1,0:T(8,128)S(1)}, u32[]{:S(2)}, u32[]{:S(2)}) collective-permute-start(f32[8,512]{1,0:T(8,128)S(1)} %get-tuple-element.105), channel_id=1, source_target_pairs={{0,4},{1,5},{2,6},{3,7},{8,12},{9,13},{10,14},{11,15},{16,20},{17,... | collective-permute-start | bytes 49160 | tf_op jit(solution)/shard_map/ppermute | solution.py:589
  126.4 6.4 %collective-permute-start.23 = (f32[8,512]{1,0:T(8,128)S(1)}, f32[8,512]{1,0:T(8,128)S(1)}, u32[]{:S(2)}, u32[]{:S(2)}) collective-permute-start(f32[8,512]{1,0:T(8,128)S(1)} %get-tuple-element.106), channel_id=1, source_target_pairs={{0,28},{1,29},{2,30},{3,31},{4,8},{5,9},{6,10},{7,11},{12,16},{13,... | collective-permute-start | bytes 49160 | tf_op jit(solution)/shard_map/ppermute | solution.py:589
  128.4 4.6 %collective-permute-start.24 = (f32[8,512]{1,0:T(8,128)S(1)}, f32[8,512]{1,0:T(8,128)S(1)}, u32[]{:S(2)}, u32[]{:S(2)}) collective-permute-start(f32[8,512]{1,0:T(8,128)S(1)} %get-tuple-element.107), channel_id=1, source_target_pairs={{0,16},{1,17},{2,18},{3,19},{4,20},{5,21},{6,22},{7,23},{8,24},{9,... | collective-permute-start | bytes 49160 | tf_op jit(solution)/shard_map/ppermute | solution.py:589
